TPU v7x, 128 devices: a whole 4x4x4 slice. The times are simulated.
128 devices in a mesh: rows: 16 (over x, z_lo, core), planes: 8 (over y, z_hi).
Axes of the slice: x: 4, y: 4, z: 4 (z_hi: 2, z_lo: 2; z = z_hi * 2 + z_lo), core: 2. Of those that a mesh axis runs over, the one named last changes fastest.
Arguments:
- density: float32 [8, 4096, 4096], P('planes', 'rows'), may hold values from -6 to 6
- lens_weight: float32 [8], P('planes'), may hold values from 0.05 to 0.5
- spectrum_bin: int32 [4096, 4096], P(None, ('rows', 'planes')), may hold values from 0 to 63, as said below
Outputs:
- shear_real: float32 [4096, 4096], P(('rows', 'planes'))
- shear_imag: float32 [4096, 4096], P(('rows', 'planes'))
- spectrum: float32 [64], replicated
Inputs may be any that keep to these rules, and one draw needn't show every extreme that they name: `spectrum_bin`: each Fourier pixel's band.
All inputs are finite; a program needn't handle non-finite values.
Results may differ from a plain program's by a relative error of at most 0.0003.
Values sent between devices are 32-bit elements; how exact they have to be, the bound alone decides.
No kernel may reach another device: no remote copies, remote signals or barrier semaphores. Data moves between devices by JAX's collectives and lax.ppermute only.
A program may use at most 64 MiB of HBM per device.

v0:
```python
from functools import partial
import math

import numpy as np
import jax
import jax.numpy as jnp
from jax import lax
from jax.experimental import pallas as pl
from jax.experimental.pallas import tpu as pltpu
from jax.sharding import Mesh
from jax.sharding import PartitionSpec as P

N = 4096
LONG = 128
SHORT = 32
NBINS = 64
ROWS = ("rows_0", "rows_1", "rows_2")
PLANES = ("planes_0", "planes_1")
ROWS_PLANES = ROWS + PLANES
FORTH = 16
BACK = 17
BF16 = jnp.bfloat16


def halves(table):
    high = table.astype(np.float32).astype(jnp.bfloat16)
    low = (table - high.astype(np.float64)).astype(np.float32).astype(jnp.bfloat16)
    return high, low


def tables():
    def wave(left, right, length):
        angle = 2.0 * np.pi * ((left[:, None] * right[None, :]) % length) / length
        return np.cos(angle), np.sin(angle)

    long_index = np.arange(LONG)
    short_index = np.arange(SHORT)
    cos_long, sin_long = wave(long_index, long_index, LONG)
    forth = np.block([[cos_long, sin_long], [-sin_long, cos_long]])
    cos_short, sin_short = wave(short_index, short_index, SHORT)
    cos_four, sin_four = np.kron(np.eye(4), cos_short), np.kron(np.eye(4), sin_short)
    short_forth = np.block([[cos_four, -sin_four], [sin_four, cos_four]])
    row_turn = wave(short_index, long_index, N)
    cos_turn, sin_turn = wave(long_index, short_index, N)
    column_turn = (np.tile(cos_turn, (1, 4)), np.tile(sin_turn, (1, 4)))
    return {
        "forth": np.concatenate(halves(forth), axis=1),
        "back": np.concatenate(halves(forth.T), axis=1),
        "short_forth": np.concatenate(halves(short_forth), axis=0),
        "short_back": np.concatenate(halves(short_forth.T), axis=0),
        "right_back": np.concatenate(halves(forth), axis=0),
        "row_turn": np.stack(row_turn).astype(np.float32),
        "column_turn": np.stack(column_turn).astype(np.float32),
    }


def plus(a, b):
    if a is None:
        return b
    if b is None:
        return a
    return a + b


def minus(a, b):
    if b is None:
        return a
    if a is None:
        return -b
    return a - b


def scaled(a, factor):
    if a is None or factor == 0.0:
        return None
    if factor == 1.0:
        return a
    if factor == -1.0:
        return -a
    return a * factor


def rotated(value, step, length, orient):
    step %= length
    quarter, rest = divmod(4 * step, length)
    real, imag = value
    if rest == 0:
        cosine = (1.0, 0.0, -1.0, 0.0)[quarter]
        sine = (0.0, 1.0, 0.0, -1.0)[quarter] * orient
    else:
        cosine = math.cos(2.0 * math.pi * step / length)
        sine = orient * math.sin(2.0 * math.pi * step / length)
    return (
        minus(scaled(real, cosine), scaled(imag, sine)),
        plus(scaled(real, sine), scaled(imag, cosine)),
    )


def transformed(values, orient):
    length = len(values)
    if length == 1:
        return values
    even = transformed(values[0::2], orient)
    odd = transformed(values[1::2], orient)
    front, rear = [], []
    for k in range(length // 2):
        turned = rotated(odd[k], k, length, orient)
        front.append((plus(even[k][0], turned[0]), plus(even[k][1], turned[1])))
        rear.append((minus(even[k][0], turned[0]), minus(even[k][1], turned[1])))
    return front + rear


def transformed_real(values):
    length = len(values)
    if length == 1:
        return [(values[0], None)]
    if length == 2:
        return [(values[0] + values[1], None), (values[0] - values[1], None)]
    even = transformed_real(values[0::2])
    odd = transformed_real(values[1::2])
    out = [None] * (length // 2 + 1)
    for k in range(length // 4 + 1):
        turned = rotated(odd[k], k, length, -1.0)
        out[k] = (plus(even[k][0], turned[0]), plus(even[k][1], turned[1]))
        mirror_imag = minus(turned[1], even[k][1])
        out[length // 2 - k] = (minus(even[k][0], turned[0]), mirror_imag)
    return out


def split(value):
    high = value.astype(BF16)
    return high, (value - high.astype(jnp.float32)).astype(BF16)


def product(left, right, dims=((1,), (0,))):
    return lax.dot_general(left, right, (dims, ((), ())), preferred_element_type=jnp.float32)


def table_times(table_ref, value):
    size = value.shape[0]
    high, low = split(value)
    stacked = jnp.concatenate([high, low, high], axis=0)
    left = jnp.concatenate([table_ref[:, :size], table_ref[:, :size], table_ref[:, size:]], axis=1)
    return product(left, stacked)


def table_times_rows(table_ref, value):
    size = value.shape[1]
    high, low = split(value)
    stacked = jnp.concatenate([high, low, high], axis=1)
    left = jnp.concatenate([table_ref[:, :size], table_ref[:, :size], table_ref[:, size:]], axis=1)
    return product(left, stacked, ((1,), (1,)))


def times_table(value, table_ref):
    size = value.shape[1]
    high, low = split(value)
    stacked = jnp.concatenate([high, low, high], axis=1)
    right = jnp.concatenate([table_ref[:size], table_ref[:size], table_ref[size:]], axis=0)
    return product(stacked, right)


def rows_forth_kernel(field_ref, turn_ref, forth_ref, out_ref, held_ref):
    for block in range(4):
        rows = slice(8 * block, 8 * block + 8)
        pieces = []
        for n in range(SHORT):
            lanes = slice(LONG * n, LONG * n + LONG)
            total = field_ref[0, rows, lanes]
            for p in range(1, field_ref.shape[0]):
                total = total + field_ref[p, rows, lanes]
            pieces.append(total)
        half = transformed_real(pieces)
        for k in range(SHORT):
            real, imag = half[k] if k <= SHORT // 2 else half[SHORT - k]
            if k > SHORT // 2:
                imag = None if imag is None else -imag
            cosine = turn_ref[0, k : k + 1, :]
            sine = turn_ref[1, k : k + 1, :]
            if imag is None:
                held_ref[k, block, :, :LONG] = real * cosine
                held_ref[k, block, :, LONG:] = -(real * sine)
            else:
                held_ref[k, block, :, :LONG] = real * cosine + imag * sine
                held_ref[k, block, :, LONG:] = imag * cosine - real * sine
    for quarter in range(4):
        rows = held_ref[8 * quarter : 8 * quarter + 8].reshape(256, 2 * LONG)
        spread = table_times_rows(forth_ref, rows)
        for part in range(2):
            for side in range(2):
                tile = 8 * part + 2 * quarter + side
                out_ref[pl.ds(tile, LONG, FORTH), :] = spread[
                    LONG * part : LONG * part + LONG, LONG * side : LONG * side + LONG
                ]


def columns_kernel(
    first_ref,
    arrived_ref,
    bins_ref,
    turn_ref,
    forth_ref,
    back_ref,
    short_forth_ref,
    short_back_ref,
    out_ref,
    power_ref,
    bands_ref,
):
    lane = lax.broadcasted_iota(jnp.int32, (LONG, LONG), 1)
    row = lax.broadcasted_iota(jnp.int32, (LONG, LONG), 0)
    height = row + LONG * (lane % SHORT)
    height = ((height + N // 2) % N - N // 2).astype(jnp.float32)
    height_square = height * height
    first = first_ref[0]
    for pair in range(4):
        columns = []
        for side in range(2):
            group = 2 * pair + side
            columns.append(
                jnp.concatenate(
                    [
                        arrived_ref[pl.ds(group, LONG, FORTH), :],
                        arrived_ref[pl.ds(8 + group, LONG, FORTH), :],
                    ],
                    axis=0,
                )
            )
        spread = table_times(forth_ref, jnp.concatenate(columns, axis=1))
        cosine = turn_ref[0]
        sine = turn_ref[1]
        turned = []
        for side in range(2):
            lanes = slice(LONG * side, LONG * side + LONG)
            real, imag = spread[:LONG, lanes], spread[LONG:, lanes]
            turned.append(
                jnp.concatenate([real * cosine + imag * sine, imag * cosine - real * sine], axis=1)
            )
        held = times_table(jnp.concatenate(turned, axis=0), short_forth_ref)
        hats = []
        for side in range(2):
            group = 2 * pair + side
            real = held[LONG * side : LONG * side + LONG, :LONG]
            imag = held[LONG * side : LONG * side + LONG, LONG:]
            across = first + 4 * group + lane // SHORT
            across = ((across + N // 2) % N - N // 2).astype(jnp.float32)
            across_square = across * across
            square_norm = height_square + across_square
            anchor = square_norm == 0.0
            real = jnp.where(anchor, 0.0, real)
            imag = jnp.where(anchor, 0.0, imag)
            power_ref[LONG * group : LONG * group + LONG, :] = real * real + imag * imag
            inverse = (1.0 / float(N) ** 2) / jnp.where(anchor, 1.0, square_norm)
            kernel_real = (across_square - height_square) * inverse
            kernel_imag = (across * height) * (2.0 * inverse)
            hats.append(
                jnp.concatenate(
                    [
                        kernel_real * real - kernel_imag * imag,
                        kernel_real * imag + kernel_imag * real,
                    ],
                    axis=1,
                )
            )
        returned = times_table(jnp.concatenate(hats, axis=0), short_back_ref)
        columns = []
        for side in range(2):
            rows = slice(LONG * side, LONG * side + LONG)
            real, imag = returned[rows, :LONG], returned[rows, LONG:]
            columns.append(
                jnp.concatenate([real * cosine - imag * sine, imag * cosine + real * sine], axis=0)
            )
        restored = table_times(back_ref, jnp.concatenate(columns, axis=1))
        for part in range(2):
            for side in range(2):
                tile = 8 * part + 2 * pair + side
                out_ref[pl.ds(tile, LONG, BACK), :] = restored[
                    LONG * part : LONG * part + LONG, LONG * side : LONG * side + LONG
                ]

    def one_block(block, carry):
        start = pl.multiple_of(block * 64, 64)
        power = power_ref[pl.ds(start, 64), :]
        bins = bins_ref[pl.ds(start, 64), :]
        for band in range(NBINS):
            chosen = jnp.where(bins == band, power, 0.0)
            bands_ref[8 * band : 8 * band + 8, :] += jnp.sum(chosen.reshape(8, 8, LONG), axis=0)
        return carry

    bands_ref[...] = jnp.zeros_like(bands_ref)
    lax.fori_loop(0, 8 * LONG // 64, one_block, 0)
    sums = jnp.sum(bands_ref[...].reshape(NBINS, 8, LONG), axis=1)
    sums = jnp.concatenate([sums, jnp.zeros((LONG - NBINS, LONG), jnp.float32)], axis=0)
    line = jnp.sum(sums.T, axis=0, keepdims=True) * (NBINS / float(N) ** 4)
    out_ref[pl.ds(16, LONG, BACK), :] = jnp.broadcast_to(line, (LONG, LONG))


def rows_back_kernel(
    arrived_ref, turn_ref, table_ref, real_ref, imag_ref, spectrum_ref, held_ref
):
    for group in range(8):
        pair = jnp.concatenate(
            [
                arrived_ref[pl.ds(group, LONG, BACK), :].T,
                arrived_ref[pl.ds(8 + group, LONG, BACK), :].T,
            ],
            axis=1,
        )
        held_ref[LONG * group : LONG * group + LONG, :] = times_table(pair, table_ref)
    spectrum_ref[...] = jnp.sum(
        arrived_ref[pl.ds(16, LONG, BACK), :], axis=0, keepdims=True
    )
    for block in range(4):
        pieces = []
        for k in range(SHORT):
            rows = slice(SHORT * k + 8 * block, SHORT * k + 8 * block + 8)
            cosine = turn_ref[0, k : k + 1, :]
            sine = turn_ref[1, k : k + 1, :]
            real, imag = held_ref[rows, :LONG], held_ref[rows, LONG:]
            pieces.append((real * cosine - imag * sine, imag * cosine + real * sine))
        for n, (real, imag) in enumerate(transformed(pieces, 1.0)):
            real_ref[8 * block : 8 * block + 8, LONG * n : LONG * n + LONG] = real
            imag_ref[8 * block : 8 * block + 8, LONG * n : LONG * n + LONG] = imag


def call(kernel, outs, scratch, inputs, name, smem_first=False):
    whole = pl.BlockSpec(memory_space=pltpu.VMEM)
    specs = [whole] * len(inputs)
    if smem_first:
        specs[0] = pl.BlockSpec(memory_space=pltpu.SMEM)
    return pl.pallas_call(
        kernel,
        out_shape=outs,
        in_specs=specs,
        out_specs=jax.tree.map(lambda _: whole, outs),
        scratch_shapes=scratch,
        name=name,
        compiler_params=pltpu.CompilerParams(vmem_limit_bytes=48 * 1024 * 1024),
    )(*inputs)


def f32(*shape):
    return jax.ShapeDtypeStruct(shape, jnp.float32)


def exchanged(array, height):
    blocks = array.reshape(LONG, 1, height * LONG)
    blocks = lax.all_to_all(blocks, ROWS_PLANES, split_axis=0, concat_axis=0, tiled=True)
    return blocks.reshape(LONG * height, LONG)


def on_device(density, lens_weight, spectrum_bin):
    held = tables()
    planes_here, slab_rows, length = density.shape
    plane_count = lax.axis_size(PLANES)
    device = lax.axis_index(ROWS_PLANES)
    weighted = density[0] * lens_weight[0]
    blocks = weighted.reshape(plane_count, slab_rows // plane_count, length)
    blocks = lax.all_to_all(blocks, PLANES, split_axis=0, concat_axis=0, tiled=True)
    bins = spectrum_bin.reshape(SHORT, LONG, 8, 4).transpose(2, 1, 3, 0).reshape(8 * LONG, LONG)
    sent = call(
        rows_forth_kernel,
        f32(LONG * FORTH, LONG),
        [pltpu.VMEM((SHORT, 4, 8, 2 * LONG), jnp.float32)],
        (blocks, held["row_turn"], held["forth"]),
        "rows_forth",
    )
    arrived = exchanged(sent, FORTH)
    sent = call(
        columns_kernel,
        f32(LONG * BACK, LONG),
        [pltpu.VMEM((8 * LONG, LONG), jnp.float32), pltpu.VMEM((8 * NBINS, LONG), jnp.float32)],
        (
            (device * SHORT).reshape(1),
            arrived,
            bins,
            held["column_turn"],
            held["forth"],
            held["back"],
            held["short_forth"],
            held["short_back"],
        ),
        "columns",
        smem_first=True,
    )
    arrived = exchanged(sent, BACK)
    shear_real, shear_imag, spectrum = call(
        rows_back_kernel,
        (f32(SHORT, N), f32(SHORT, N), f32(1, LONG)),
        [pltpu.VMEM((8 * LONG, 2 * LONG), jnp.float32)],
        (arrived, held["row_turn"], held["right_back"]),
        "rows_back",
    )
    return shear_real, shear_imag, spectrum[0, :NBINS]


def solution(mesh):
    finer = Mesh(mesh.devices.reshape(4, 2, 2, 4, 2), ROWS_PLANES)
    in_specs = (P(PLANES, ROWS, None), P(PLANES), P(None, ROWS_PLANES))
    out_specs = (P(ROWS_PLANES, None), P(ROWS_PLANES, None), P())
    return jax.shard_map(
        on_device, mesh=finer, in_specs=in_specs, out_specs=out_specs, check_vma=False
    )
```

profile of v0, /device:TPU:1, one launch (start us, length us, event | category | flops | bytes accessed | tf_op | source)
XLA Modules:
  0.0 124.6 jit_solution(7345924921992336201)
XLA Ops:
  1.3 2.5 %broadcast_multiply_fusion = f32[1,256,4096]{2,1,0:T(8,128)S(1)} fusion(f32[1,256,4096]{2,1,0:T(8,128)} %param.10, f32[]{:T(128)} %bitcast.22), kind=kLoop, calls=%fused_computation | loop fusion | flops 1048576 | bytes 8388612 | tf_op jit(solution)/shard_map/mul | solution.py:357
  3.7 0.0 copy-start
  3.8 0.0 copy-start.5
  3.8 57.5 %all_to_all.15.field_ref = f32[8,32,4096]{2,1,0:T(8,128)S(1)} all-to-all(f32[8,32,4096]{2,1,0:T(8,128)S(1)} %bitcast.26), channel_id=1, replica_groups=mesh['rows_0'=4,'rows_1'=2,'rows_2'=2,'planes_0'=4,'planes_1'=2] {'plane..., dimensions={0} | all-to-all | bytes 8388608 | tf_op jit(solution)/shard_map/all_to_all | solution.py:359
  61.3 0.0 copy-done
  61.3 0.0 copy-done.5
  61.3 0.0 copy-start.7
  61.3 2.1 %rows_forth.1 = f32[2048,128]{1,0:T(8,128)} custom-call(f32[8,32,4096]{2,1,0:T(8,128)S(1)} %all_to_all.15.field_ref, f32[2,32,128]{2,1,0:T(8,128)S(1)} %copy-done.5, bf16[256,512]{1,0:T(8,128)(2,1)S(1)} %copy-done), custom_call_target="tpu_custom_call" | custom-call | tf_op jit(solution)/shard_map/rows_forth/pallas_call | solution.py:331
  63.4 0.0 copy-start.1
  63.4 0.0 copy-start.2
  63.4 0.0 copy-start.3
  63.4 0.0 copy-start.6
  63.4 8.1 %all-to-all-start.1 = ((f32[128,1,2048]{2,1,0:T(1,128)}), f32[128,1,2048]{2,1,0:T(1,128)S(1)}, u32[]{:S(2)}, u32[]{:S(2)}) async-start(f32[128,1,2048]{2,1,0:T(1,128)} %bitcast.3), calls=%async_computation.1 | async-start | bytes 2097152 | tf_op jit(solution)/shard_map/all_to_all | solution.py:348
  71.6 0.0 copy-done.7
  71.6 0.1 copy.20
  71.7 0.3 copy.17
  72.0 0.0 copy-start.4
  72.0 0.9 copy.23
  72.9 1.2 copy.18.bins_ref
  74.1 16.9 %all-to-all-done.1 = f32[128,1,2048]{2,1,0:T(1,128)S(1)} async-done(((f32[128,1,2048]{2,1,0:T(1,128)}), f32[128,1,2048]{2,1,0:T(1,128)S(1)}, u32[]{:S(2)}, u32[]{:S(2)}) %all-to-all-start.1) | async-done | bytes 1048608 | tf_op jit(solution)/shard_map/all_to_all | solution.py:348
  91.0 0.0 copy-done.1
  91.0 0.0 copy-done.2
  91.0 0.0 copy-done.3
  91.0 0.0 copy-done.6
  91.0 7.3 %columns.1 = f32[2176,128]{1,0:T(8,128)S(1)} custom-call(s32[1]{0:T(128)} %bitcast.first_ref, f32[2048,128]{1,0:T(8,128)S(1)} %bitcast.25, s32[1024,128]{1,0:T(8,128)S(1)} %copy.18.bins_ref, f32[2,128,128]{2,1,0:T(8,128)S(1)} %copy-done.6, bf16[256,512]{1,0:T(8,128)(2,1)S(1)} %copy-done, bf16[256,512]{1,0:T(8,128)(2,1)S(1)} %copy-done.1, ...), custom_call_target="tpu_custom_call" | custom-call | tf_op jit(solution)/shard_map/columns/pallas_call | solution.py:331
  98.3 23.9 %all_to_all.16 = f32[128,1,2176]{2,1,0:T(1,128)S(1)} all-to-all(f32[128,1,2176]{2,1,0:T(1,128)S(1)} %bitcast.23), channel_id=1, replica_groups=mesh['rows_0'=4,'rows_1'=2,'rows_2'=2,'planes_0'=4,'planes_1'=2] {'rows_..., dimensions={0} | all-to-all | bytes 2228224 | tf_op jit(solution)/shard_map/all_to_all | solution.py:348
  122.2 0.0 copy-done.4
  122.2 1.9 %rows_back.1 = (f32[32,4096]{1,0:T(8,128)}, f32[32,4096]{1,0:T(8,128)}, f32[1,128]{1,0:T(1,128)S(1)}) custom-call(f32[2176,128]{1,0:T(8,128)S(1)} %bitcast.24, f32[2,32,128]{2,1,0:T(8,128)S(1)} %copy-done.5, bf16[512,256]{1,0:T(8,128)(2,1)S(1)} %copy-done.4), custom_call_target="tpu_custom_call" | custom-call | tf_op jit(solution)/shard_map/rows_back/pallas_call | solution.py:331
  124.1 0.5 slice_bitcast_fusion
Async XLA Ops:
  3.7 57.6 %copy-start = (bf16[256,512]{1,0:T(8,128)(2,1)S(1)}, bf16[256,512]{1,0:T(8,128)(2,1)}, u32[]{:S(2)}) copy-start(bf16[256,512]{1,0:T(8,128)(2,1)} %constant.42.clone.forth_ref) | copy-start | bytes 786436
  3.8 57.6 %copy-start.5 = (f32[2,32,128]{2,1,0:T(8,128)S(1)}, f32[2,32,128]{2,1,0:T(8,128)}, u32[]{:S(2)}) copy-start(f32[2,32,128]{2,1,0:T(8,128)} %constant.41.clone.turn_ref) | copy-start | bytes 98308
  61.3 10.2 %copy-start.7 = (s32[4096,32]{0,1:T(8,128)S(1)}, s32[4096,32]{0,1:T(8,128)}, u32[]{:S(2)}) copy-start(s32[4096,32]{0,1:T(8,128)} %param.12) | copy-start | bytes 1572868
  63.4 27.6 %copy-start.1 = (bf16[256,512]{1,0:T(8,128)(2,1)S(1)}, bf16[256,512]{1,0:T(8,128)(2,1)}, u32[]{:S(2)}) copy-start(bf16[256,512]{1,0:T(8,128)(2,1)} %constant.44.clone.back_ref) | copy-start | bytes 786436
  63.4 27.6 %copy-start.2 = (bf16[512,256]{1,0:T(8,128)(2,1)S(1)}, bf16[512,256]{1,0:T(8,128)(2,1)}, u32[]{:S(2)}) copy-start(bf16[512,256]{1,0:T(8,128)(2,1)} %constant.45.clone.short_forth_ref) | copy-start | bytes 786436
  63.4 27.6 %copy-start.3 = (bf16[512,256]{1,0:T(8,128)(2,1)S(1)}, bf16[512,256]{1,0:T(8,128)(2,1)}, u32[]{:S(2)}) copy-start(bf16[512,256]{1,0:T(8,128)(2,1)} %constant.46.clone.short_back_ref) | copy-start | bytes 786436
  63.4 27.6 %copy-start.6 = (f32[2,128,128]{2,1,0:T(8,128)S(1)}, f32[2,128,128]{2,1,0:T(8,128)}, u32[]{:S(2)}) copy-start(f32[2,128,128]{2,1,0:T(8,128)} %constant.43.clone.turn_ref) | copy-start | bytes 393220
  63.4 27.6 %all-to-all-start.1 = ((f32[128,1,2048]{2,1,0:T(1,128)}), f32[128,1,2048]{2,1,0:T(1,128)S(1)}, u32[]{:S(2)}, u32[]{:S(2)}) async-start(f32[128,1,2048]{2,1,0:T(1,128)} %bitcast.3), calls=%async_computation.1 | async-start | bytes 2097152 | tf_op jit(solution)/shard_map/all_to_all | solution.py:348
  72.0 50.2 %copy-start.4 = (bf16[512,256]{1,0:T(8,128)(2,1)S(1)}, bf16[512,256]{1,0:T(8,128)(2,1)}, u32[]{:S(2)}) copy-start(bf16[512,256]{1,0:T(8,128)(2,1)} %constant.47.clone.table_ref) | copy-start | bytes 786436
where the time goes:
time: 125 us
  blocking collectives  81.4 us (65%)
  waiting for transfers between devices  16.9 us (14%)
  Pallas kernels  11.2 us (9%)
  starting transfers between devices  8.13 us (7%)
  local copies, waits for them, and re-layouts  3.07 us (2%)
  other arithmetic  2.46 us (2%)
  between operations  1.38 us (1%)
    all_to_all x1, blocking collectives, on_device(): lax.all_to_all(blocks, PLANES, split_axis=0, concat_axis=0, tiled=True)  57.5 us
    all_to_all x1, blocking collectives, exchanged(): lax.all_to_all(blocks, ROWS_PLANES, split_axis=0, concat_axis=0, tiled=True)  23.9 us
    all_to_all x1, waiting for transfers between devices, exchanged(): lax.all_to_all(blocks, ROWS_PLANES, split_axis=0, concat_axis=0, tiled=True)  16.9 us
    pallas_call x3, Pallas kernels, call(): pl.pallas_call(kernel, out_shape=outs, in_specs=specs, out_specs=jax.tree...  11.2 us
    all_to_all x1, starting transfers between devices, exchanged(): lax.all_to_all(blocks, ROWS_PLANES, split_axis=0, concat_axis=0, tiled=True)  8.13 us
  transfers between devices with their start and end apart: 1, of which 1 were waited for; matrix products, arithmetic and copies ran while one was open for 2% of the time, Pallas kernels for 0%

commit v1 on v0

--- a/solution.py
+++ b/solution.py
@@ -1,4 +1,3 @@
-from functools import partial
 import math
 
 import numpy as np
@@ -9,6 +8,7 @@
 from jax.experimental.pallas import tpu as pltpu
 from jax.sharding import Mesh
 from jax.sharding import PartitionSpec as P
+
 
 N = 4096
 LONG = 128
@@ -19,6 +19,8 @@
 ROWS_PLANES = ROWS + PLANES
 FORTH = 16
 BACK = 17
+EARLY_HALF = 1280
+EARLY = 2 * EARLY_HALF
 BF16 = jnp.bfloat16
 
 
@@ -160,15 +162,18 @@
     return product(stacked, right)
 
 
-def rows_forth_kernel(field_ref, turn_ref, forth_ref, out_ref, held_ref):
+def rows_forth_kernel(*refs):
+    field_refs = refs[:6]
+    turn_ref, forth_ref, out_ref, held_ref = refs[6:]
     for block in range(4):
         rows = slice(8 * block, 8 * block + 8)
         pieces = []
         for n in range(SHORT):
-            lanes = slice(LONG * n, LONG * n + LONG)
-            total = field_ref[0, rows, lanes]
-            for p in range(1, field_ref.shape[0]):
-                total = total + field_ref[p, rows, lanes]
+            terms, start = part_terms(field_refs, LONG * n)
+            lanes = slice(LONG * n - start, LONG * n - start + LONG)
+            total = terms[0][rows, lanes]
+            for term in terms[1:]:
+                total = total + term[rows, lanes]
             pieces.append(total)
         half = transformed_real(pieces)
         for k in range(SHORT):
@@ -192,6 +197,12 @@
                 out_ref[pl.ds(tile, LONG, FORTH), :] = spread[
                     LONG * part : LONG * part + LONG, LONG * side : LONG * side + LONG
                 ]
+
+
+def part_terms(refs, column):
+    if column < EARLY:
+        return refs[:2], 0
+    return refs[2:6], EARLY
 
 
 def columns_kernel(
@@ -307,9 +318,8 @@
             axis=1,
         )
         held_ref[LONG * group : LONG * group + LONG, :] = times_table(pair, table_ref)
-    spectrum_ref[...] = jnp.sum(
-        arrived_ref[pl.ds(16, LONG, BACK), :], axis=0, keepdims=True
-    )
+    bands = jnp.sum(arrived_ref[pl.ds(16, LONG, BACK), :], axis=0, keepdims=True)
+    spectrum_ref[...] = bands[:, :NBINS]
     for block in range(4):
         pieces = []
         for k in range(SHORT):
@@ -323,7 +333,7 @@
             imag_ref[8 * block : 8 * block + 8, LONG * n : LONG * n + LONG] = imag
 
 
-def call(kernel, outs, scratch, inputs, name, smem_first=False):
+def call(kernel, outs, scratch, inputs, smem_first=False):
     whole = pl.BlockSpec(memory_space=pltpu.VMEM)
     specs = [whole] * len(inputs)
     if smem_first:
@@ -334,7 +344,6 @@
         in_specs=specs,
         out_specs=jax.tree.map(lambda _: whole, outs),
         scratch_shapes=scratch,
-        name=name,
         compiler_params=pltpu.CompilerParams(vmem_limit_bytes=48 * 1024 * 1024),
     )(*inputs)
 
@@ -349,21 +358,100 @@
     return blocks.reshape(LONG * height, LONG)
 
 
+def along(array, step):
+    return lax.ppermute(array, PLANES[0], [(i, (i + step) % 4) for i in range(4)])
+
+
+def swapped(array):
+    return lax.ppermute(array, PLANES[1], [(0, 1), (1, 0)])
+
+
+def apart(array):
+    return lax.optimization_barrier(array)
+
+
+def added_kernel(index_ref, scale_ref, own_ref, far_ref, out_ref):
+    out_ref[...] = own_ref[0] * scale_ref[0] + far_ref[...]
+
+
+def added(index, scale, whole, side, far):
+    shape = (1,) + far.shape
+    lead = (0,) * (len(shape) - 2)
+    here = lambda i, index_ref: (index_ref[0],) + lead + (side,)
+    rest = lambda i, index_ref: lead + (0,)
+    grid_spec = pltpu.PrefetchScalarGridSpec(
+        num_scalar_prefetch=1,
+        grid=(1,),
+        in_specs=[
+            pl.BlockSpec(memory_space=pltpu.SMEM),
+            pl.BlockSpec(shape, here),
+            pl.BlockSpec(far.shape, rest),
+        ],
+        out_specs=pl.BlockSpec(far.shape, rest),
+    )
+    return pl.pallas_call(
+        added_kernel, grid_spec=grid_spec, out_shape=f32(*far.shape), name="added"
+    )(index.reshape(1), scale.reshape(1), whole, far)
+
+
+def summed_along(piece, bound):
+    far_up = along(piece(2, 0), 1)
+    far_down = along(piece(2, 1), -1)
+    up_free = along(piece(1, 1), 1)
+    down_free = along(piece(-1, 0), -1)
+    up_bound = along(bound(1, 0, far_up), 1)
+    down_bound = along(bound(-1, 1, far_down), -1)
+    return (up_bound, down_free), (up_free, down_bound)
+
+
+def plane_sum(density, weight):
+    length = density.shape[-1]
+    here = lax.axis_index(PLANES[0])
+    upper = lax.axis_index(PLANES[1])
+    blocks = density.reshape(4, 2, -1, length)
+    rows = blocks.shape[2]
+
+    def early(step, side):
+        got = lax.dynamic_slice(
+            blocks, ((here + step) & 3, 0, 0, side * EARLY_HALF), (1, 2, rows, EARLY_HALF)
+        )
+        return got[0] * weight
+
+    def early_bound(step, side, far):
+        return added((here + step) & 3, weight, blocks, side, far)
+
+    def late_block(half):
+        got = lax.dynamic_slice(
+            blocks, (0, half, 0, EARLY), (4, 1, rows, length - EARLY)
+        )
+        return got[:, 0] * weight
+
+    late_other = swapped(late_block(1 - upper))
+    left, right = summed_along(early, early_bound)
+    late = apart(late_block(upper) + late_other)
+
+    def late_piece(step):
+        return lax.dynamic_index_in_dim(late, (here + step) & 3, 0, keepdims=False)
+
+    early_sum = jnp.concatenate(
+        [early(0, 0) + left[0] + left[1], early(0, 1) + right[0] + right[1]], axis=-1
+    )
+    mine = lax.dynamic_index_in_dim(early_sum, upper, 0, keepdims=False)
+    other = swapped(lax.dynamic_index_in_dim(early_sum, 1 - upper, 0, keepdims=False))
+    late_terms = [along(late_piece(step), step) for step in (1, -1, 2)]
+    return (mine, other, late_piece(0), *late_terms)
+
+
 def on_device(density, lens_weight, spectrum_bin):
     held = tables()
-    planes_here, slab_rows, length = density.shape
-    plane_count = lax.axis_size(PLANES)
     device = lax.axis_index(ROWS_PLANES)
-    weighted = density[0] * lens_weight[0]
-    blocks = weighted.reshape(plane_count, slab_rows // plane_count, length)
-    blocks = lax.all_to_all(blocks, PLANES, split_axis=0, concat_axis=0, tiled=True)
+    parts = plane_sum(density[0], lens_weight[0])
     bins = spectrum_bin.reshape(SHORT, LONG, 8, 4).transpose(2, 1, 3, 0).reshape(8 * LONG, LONG)
     sent = call(
         rows_forth_kernel,
         f32(LONG * FORTH, LONG),
         [pltpu.VMEM((SHORT, 4, 8, 2 * LONG), jnp.float32)],
-        (blocks, held["row_turn"], held["forth"]),
-        "rows_forth",
+        (*parts, held["row_turn"], held["forth"]),
     )
     arrived = exchanged(sent, FORTH)
     sent = call(
@@ -380,18 +468,16 @@
             held["short_forth"],
             held["short_back"],
         ),
-        "columns",
         smem_first=True,
     )
     arrived = exchanged(sent, BACK)
     shear_real, shear_imag, spectrum = call(
         rows_back_kernel,
-        (f32(SHORT, N), f32(SHORT, N), f32(1, LONG)),
+        (f32(SHORT, N), f32(SHORT, N), f32(1, NBINS)),
         [pltpu.VMEM((8 * LONG, 2 * LONG), jnp.float32)],
         (arrived, held["row_turn"], held["right_back"]),
-        "rows_back",
-    )
-    return shear_real, shear_imag, spectrum[0, :NBINS]
+    )
+    return shear_real, shear_imag, spectrum[0]
 
 
 def solution(mesh):

time: 125 us -> 121 us (0.968)
  blocking collectives: 81.4 us -> 23.9 us
  starting transfers between devices: 8.13 us -> 33.7 us
  waiting for transfers between devices: 16.9 us -> 38 us
  Pallas kernels: 11.2 us -> 14.8 us
  other arithmetic: 2.46 us -> 5.19 us
    all_to_all x1 -> x0, blocking collectives: 57.5 us -> none  [on_device(): lax.all_to_all(blocks, PLANES, split_axis=0, concat_axis=0, tiled=True)]
    ppermute x0 -> x11, waiting for transfers between devices: none -> 21.1 us  [the longest x2 11.6 us: swapped(): return lax.ppermute(array, PLANES[1], [(0, 1), (1, 0)])]
    ppermute x0 -> x11, starting transfers between devices: none -> 18 us  [the longest x9 10.8 us: along(): lax.ppermute(array, PLANES[0], [(i, (i + step) % 4) for i in range(4)])]
    all_to_all x1, starting transfers between devices: 8.13 us -> 15.7 us  [exchanged(): lax.all_to_all(blocks, ROWS_PLANES, split_axis=0, concat_axis=0, tiled=True)]
    pallas_call x0 -> x2, Pallas kernels: none -> 3.65 us  [added(): pl.pallas_call(added_kernel, grid_spec=grid_spec, out_shape=f32(*far.shap...]
    add x0 -> x2, other arithmetic: none -> 2.55 us  [the longest x1 1.28 us: plane_sum(): late = apart(late_block(upper) + late_other)]
    unnamed x18 -> x22, local copies, waits for them, and re-layouts: 1.02 us -> 2.48 us
    mul x1 -> x2, other arithmetic: 2.46 us -> 2.58 us  [the longest x1 1.39 us: early(): return got[0] * weight]
  transfers between devices with their start and end apart: 1 -> 12, of which waited for: 1 -> 7; matrix products, arithmetic and copies ran while one was open for 2% -> 5% of each run, Pallas kernels for 0% -> 3%
where the time goes in v1:
time: 121 us
  waiting for transfers between devices  38 us (31%)
  starting transfers between devices  33.7 us (28%)
  blocking collectives  23.9 us (20%)
  Pallas kernels  14.8 us (12%)
  other arithmetic  5.19 us (4%)
  local copies, waits for them, and re-layouts  4.08 us (3%)
  between operations  1.47 us (1%)
    all_to_all x1, blocking collectives, exchanged(): lax.all_to_all(blocks, ROWS_PLANES, split_axis=0, concat_axis=0, tiled=True)  23.9 us
    all_to_all x1, waiting for transfers between devices, exchanged(): lax.all_to_all(blocks, ROWS_PLANES, split_axis=0, concat_axis=0, tiled=True)  16.9 us
    all_to_all x1, starting transfers between devices, exchanged(): lax.all_to_all(blocks, ROWS_PLANES, split_axis=0, concat_axis=0, tiled=True)  15.7 us
    ppermute x2, waiting for transfers between devices, swapped(): return lax.ppermute(array, PLANES[1], [(0, 1), (1, 0)])  11.6 us
    pallas_call x3, Pallas kernels, call(): pl.pallas_call(kernel, out_shape=outs, in_specs=specs, out_specs=jax.tree...  11.1 us
    ppermute x9, starting transfers between devices, along(): lax.ppermute(array, PLANES[0], [(i, (i + step) % 4) for i in range(4)])  10.8 us
    ppermute x9, waiting for transfers between devices, along(): lax.ppermute(array, PLANES[0], [(i, (i + step) % 4) for i in range(4)])  9.53 us
    ppermute x2, starting transfers between devices, swapped(): return lax.ppermute(array, PLANES[1], [(0, 1), (1, 0)])  7.12 us
  transfers between devices with their start and end apart: 12, of which 7 were waited for; matrix products, arithmetic and copies ran while one was open for 5% of the time, Pallas kernels for 3%

profile of v1, /device:TPU:1, one launch (start us, length us, event | category | flops | bytes accessed | tf_op | source)
XLA Modules:
  0.0 121.1 jit_solution(5300724272055165628)
XLA Ops:
  1.3 1.4 %multiply_bitcast_fusion.1 = (f32[2,32,1280]{2,1,0:T(8,128)S(1)}, f32[2,32,1280]{2,1,0:T(8,128)S(1)}, f32[2,32,1280]{2,1,0:T(8,128)S(1)}, f32[2,32,1280]{2,1,0:T(8,128)S(1)}) fusion(f32[4,2,32,4096]{3,2,1,0:T(8,128)} %bitcast.74, s32[]{:T(128)S(6)} %select_n.31, f32[]{:T(128)} %bitcast.67, s32[]{:T(128)S(6)} %select_n.29, s32[]{:T(128)S(6)} %select_n.30), kind=kLoop, calls=%fused_computation.19 | loop fusion | flops 327680 | bytes 2621456 | tf_op jit(solution)/shard_map/mul | solution.py:418
  2.7 2.2 %collective-permute-start = (f32[2,32,1280]{2,1,0:T(8,128)S(1)}, f32[2,32,1280]{2,1,0:T(8,128)S(1)}, u32[]{:S(2)}, u32[]{:S(2)}) collective-permute-start(f32[2,32,1280]{2,1,0:T(8,128)S(1)} %get-tuple-element.14), channel_id=1, source_target_pairs={{0,2},{2,4},{4,6},{6,0},{1,3},{3,5},{5,7},{7,1},{8,10},{10,12},{12... | collective-permute-start | bytes 983048 | tf_op jit(solution)/shard_map/ppermute | solution.py:362
  4.9 1.5 %collective-permute-start.4 = (f32[2,32,1280]{2,1,0:T(8,128)S(1)}, f32[2,32,1280]{2,1,0:T(8,128)S(1)}, u32[]{:S(2)}, u32[]{:S(2)}) collective-permute-start(f32[2,32,1280]{2,1,0:T(8,128)S(1)} %get-tuple-element.12), channel_id=1, source_target_pairs={{0,6},{2,0},{4,2},{6,4},{1,7},{3,1},{5,3},{7,5},{8,14},{10,8},{12,... | collective-permute-start | bytes 983048 | tf_op jit(solution)/shard_map/ppermute | solution.py:362
  6.4 1.4 %collective-permute-start.2 = (f32[2,32,1280]{2,1,0:T(8,128)S(1)}, f32[2,32,1280]{2,1,0:T(8,128)S(1)}, u32[]{:S(2)}, u32[]{:S(2)}) collective-permute-start(f32[2,32,1280]{2,1,0:T(8,128)S(1)} %get-tuple-element.13), channel_id=1, source_target_pairs={{0,6},{2,0},{4,2},{6,4},{1,7},{3,1},{5,3},{7,5},{8,14},{10,8},{12,... | collective-permute-start | bytes 983048 | tf_op jit(solution)/shard_map/ppermute | solution.py:362
  7.8 5.8 %collective-permute-done.far_ref = f32[2,32,1280]{2,1,0:T(8,128)S(1)} collective-permute-done((f32[2,32,1280]{2,1,0:T(8,128)S(1)}, f32[2,32,1280]{2,1,0:T(8,128)S(1)}, u32[]{:S(2)}, u32[]{:S(2)}) %collective-permute-start) | collective-permute-done | bytes 327712 | tf_op jit(solution)/shard_map/ppermute | solution.py:362
  13.6 0.7 copy-done.9
  14.3 1.8 %added.2 = f32[2,32,1280]{2,1,0:T(8,128)} custom-call(s32[1]{0:T(128)} %bitcast.4.index_ref, f32[1]{0:T(128)} %copy.31.scale_ref, f32[4,2,32,4096]{3,2,1,0:T(8,128)} %bitcast.75, f32[2,32,1280]{2,1,0:T(8,128)} %copy-done.9), custom_call_target="tpu_custom_call" | custom-call | tf_op jit(solution)/shard_map/added/pallas_call | solution.py:392
  16.2 0.7 copy-done.8
  16.9 1.8 %added.3 = f32[2,32,1280]{2,1,0:T(8,128)} custom-call(s32[1]{0:T(128)} %bitcast.9.index_ref, f32[1]{0:T(128)} %copy.31.scale_ref, f32[4,2,32,4096]{3,2,1,0:T(8,128)} %bitcast.76, f32[2,32,1280]{2,1,0:T(8,128)} %copy-done.8), custom_call_target="tpu_custom_call" | custom-call | tf_op jit(solution)/shard_map/added/pallas_call | solution.py:392
  18.7 2.7 %collective-permute-start.5 = (f32[2,32,1280]{2,1,0:T(8,128)}, f32[2,32,1280]{2,1,0:T(8,128)}, u32[]{:S(2)}, u32[]{:S(2)}) collective-permute-start(f32[2,32,1280]{2,1,0:T(8,128)} %added.3), channel_id=1, source_target_pairs={{0,6},{2,0},{4,2},{6,4},{1,7},{3,1},{5,3},{7,5},{8,14},{10,8},{12,... | collective-permute-start | bytes 983048 | tf_op jit(solution)/shard_map/ppermute | solution.py:362
  21.4 1.2 fusion.2
  22.6 3.6 %collective-permute-start.7 = (f32[4,32,1536]{2,1,0:T(8,128)S(1)}, f32[4,32,1536]{2,1,0:T(8,128)S(1)}, u32[]{:S(2)}, u32[]{:S(2)}) collective-permute-start(f32[4,32,1536]{2,1,0:T(8,128)S(1)} %fusion.2), channel_id=1, source_target_pairs={{0,1},{1,0},{2,3},{3,2},{4,5},{5,4},{6,7},{7,6},{8,9},{9,8},{10,11... | collective-permute-start | bytes 2359304 | tf_op jit(solution)/shard_map/ppermute | solution.py:366
  26.2 1.0 collective-permute-done.1
  27.2 1.3 %fusion.7 = (f32[2,32,1280]{2,1,0:T(8,128)S(1)}, f32[2,32,1280]{2,1,0:T(8,128)S(1)}) fusion(f32[2,32,1280]{2,1,0:T(8,128)} %collective-permute-done.5, f32[2,32,1280]{2,1,0:T(8,128)S(1)} %collective-permute-done.3, f32[4,2,32,4096]{3,2,1,0:T(8,128)} %bitcast.78, s32[]{:T(128)S(6)} %select_n.28, f32[]{:T(128)} %bitcast.70, ...), kind=kLoop, calls=%fused_computation.15 | loop fusion | flops 491520 | bytes 2621448 | tf_op jit(solution)/shard_map/add | solution.py:437
  28.5 3.6 %collective-permute-start.6 = (f32[32,2560]{1,0:T(8,128)S(1)}, f32[32,2560]{1,0:T(8,128)S(1)}, u32[]{:S(2)}, u32[]{:S(2)}) collective-permute-start(f32[32,2560]{1,0:T(8,128)S(1)} %get-tuple-element.19), channel_id=1, source_target_pairs={{0,1},{1,0},{2,3},{3,2},{4,5},{5,4},{6,7},{7,6},{8,9},{9,8},{10,11... | collective-permute-start | bytes 983048 | tf_op jit(solution)/shard_map/ppermute | solution.py:366
  32.0 9.0 %collective-permute-done.7 = f32[4,32,1536]{2,1,0:T(8,128)S(1)} collective-permute-done((f32[4,32,1536]{2,1,0:T(8,128)S(1)}, f32[4,32,1536]{2,1,0:T(8,128)S(1)}, u32[]{:S(2)}, u32[]{:S(2)}) %collective-permute-start.7) | collective-permute-done | bytes 786464 | tf_op jit(solution)/shard_map/ppermute | solution.py:366
  41.0 1.3 %fusion.1 = f32[4,32,1536]{2,1,0:T(8,128)S(1)} fusion(f32[4,32,1536]{2,1,0:T(8,128)S(1)} %collective-permute-done.7, f32[4,2,32,4096]{3,2,1,0:T(8,128)} %bitcast.79, s32[]{:T(128)S(6)} %select_n.32, f32[]{:T(128)} %bitcast.68), kind=kLoop, calls=%fused_computation.2 | loop fusion | flops 393216 | bytes 2359304 | tf_op jit(solution)/shard_map/add | solution.py:431
  42.4 0.3 collective-permute-start.10
  42.7 0.4 collective-permute-start.8
  43.1 2.3 %collective-permute-start.9 = (f32[32,1536]{1,0:T(8,128)S(1)}, f32[32,1536]{1,0:T(8,128)S(1)}, u32[]{:S(2)}, u32[]{:S(2)}) collective-permute-start(f32[32,1536]{1,0:T(8,128)S(1)} %get-tuple-element.16), channel_id=1, source_target_pairs={{0,6},{2,0},{4,2},{6,4},{1,7},{3,1},{5,3},{7,5},{8,14},{10,8},{12,... | collective-permute-start | bytes 589832 | tf_op jit(solution)/shard_map/ppermute | solution.py:362
  45.4 2.7 %collective-permute-done.6.refs_1_ = f32[32,2560]{1,0:T(8,128)S(1)} collective-permute-done((f32[32,2560]{1,0:T(8,128)S(1)}, f32[32,2560]{1,0:T(8,128)S(1)}, u32[]{:S(2)}, u32[]{:S(2)}) %collective-permute-start.6) | collective-permute-done | bytes 327712 | tf_op jit(solution)/shard_map/ppermute | solution.py:366
  48.0 0.8 collective-permute-done.10.refs_5_
  48.8 2.0 %collective-permute-done.8.refs_3_ = f32[32,1536]{1,0:T(8,128)S(1)} collective-permute-done((f32[32,1536]{1,0:T(8,128)S(1)}, f32[32,1536]{1,0:T(8,128)S(1)}, u32[]{:S(2)}, u32[]{:S(2)}) %collective-permute-start.8) | collective-permute-done | bytes 196640 | tf_op jit(solution)/shard_map/ppermute | solution.py:362
  50.9 2.0 %shard_map.121 = f32[2048,128]{1,0:T(8,128)} custom-call(f32[32,2560]{1,0:T(8,128)S(1)} %get-tuple-element.20.refs_0_, f32[32,2560]{1,0:T(8,128)S(1)} %collective-permute-done.6.refs_1_, f32[32,1536]{1,0:T(8,128)S(1)} %get-tuple-element.18.refs_2_, f32[32,1536]{1,0:T(8,128)S(1)} %collective-permute-done.8.refs_3_, ...), custom_call_target="tpu_custom_call" | custom-call | tf_op jit(solution)/shard_map/pallas_call | solution.py:341
  52.9 15.7 %all-to-all-start = ((f32[128,1,2048]{2,1,0:T(1,128)}), f32[128,1,2048]{2,1,0:T(1,128)S(1)}, u32[]{:S(2)}, u32[]{:S(2)}) async-start(f32[128,1,2048]{2,1,0:T(1,128)} %bitcast.20), calls=%async_computation | async-start | bytes 2097152 | tf_op jit(solution)/shard_map/all_to_all | solution.py:357
  68.7 0.3 copy.23
  69.0 0.9 copy.30
  69.9 1.2 %copy.24.bins_ref = s32[1024,128]{1,0:T(8,128)S(1)} copy(s32[1024,128]{0,1:T(8,128)} %bitcast.81) | data formatting | bytes 1048576 | tf_op jit(solution)/shard_map/reshape | solution.py:449
  71.2 16.9 %all-to-all-done = f32[128,1,2048]{2,1,0:T(1,128)S(1)} async-done(((f32[128,1,2048]{2,1,0:T(1,128)}), f32[128,1,2048]{2,1,0:T(1,128)S(1)}, u32[]{:S(2)}, u32[]{:S(2)}) %all-to-all-start) | async-done | bytes 1048608 | tf_op jit(solution)/shard_map/all_to_all | solution.py:357
  88.1 7.3 %shard_map.122 = f32[2176,128]{1,0:T(8,128)S(1)} custom-call(s32[1]{0:T(128)} %bitcast.first_ref, f32[2048,128]{1,0:T(8,128)S(1)} %bitcast.73, s32[1024,128]{1,0:T(8,128)S(1)} %copy.24.bins_ref, f32[2,128,128]{2,1,0:T(8,128)S(1)} %copy-done.6, bf16[256,512]{1,0:T(8,128)(2,1)S(1)} %copy-done, bf16[256,512]{1,0:T(8,128)(2,1)S(1)} %copy-done.1, ...), custom_call_target="tpu_custom_call" | custom-call | tf_op jit(solution)/shard_map/pallas_call | solution.py:341
  95.4 23.9 %all_to_all.10 = f32[128,1,2176]{2,1,0:T(1,128)S(1)} all-to-all(f32[128,1,2176]{2,1,0:T(1,128)S(1)} %bitcast.71), channel_id=1, replica_groups=mesh['rows_0'=4,'rows_1'=2,'rows_2'=2,'planes_0'=4,'planes_1'=2] {'rows_..., dimensions={0} | all-to-all | bytes 2228224 | tf_op jit(solution)/shard_map/all_to_all | solution.py:357
  119.3 1.9 %shard_map.123 = (f32[32,4096]{1,0:T(8,128)}, f32[32,4096]{1,0:T(8,128)}, f32[1,64]{1,0:T(1,128)}) custom-call(f32[2176,128]{1,0:T(8,128)S(1)} %bitcast.72, f32[2,32,128]{2,1,0:T(8,128)S(1)} %copy-done.5, bf16[512,256]{1,0:T(8,128)(2,1)S(1)} %copy-done.4), custom_call_target="tpu_custom_call" | custom-call | tf_op jit(solution)/shard_map/pallas_call | solution.py:341
  (28 shorter events, 0.4 us)
Async XLA Ops:
  2.7 10.9 %collective-permute-start = (f32[2,32,1280]{2,1,0:T(8,128)S(1)}, f32[2,32,1280]{2,1,0:T(8,128)S(1)}, u32[]{:S(2)}, u32[]{:S(2)}) collective-permute-start(f32[2,32,1280]{2,1,0:T(8,128)S(1)} %get-tuple-element.14), channel_id=1, source_target_pairs={{0,2},{2,4},{4,6},{6,0},{1,3},{3,5},{5,7},{7,1},{8,10},{10,12},{12... | collective-permute-start | bytes 983048 | tf_op jit(solution)/shard_map/ppermute | solution.py:362
  4.9 11.3 %collective-permute-start.4 = (f32[2,32,1280]{2,1,0:T(8,128)S(1)}, f32[2,32,1280]{2,1,0:T(8,128)S(1)}, u32[]{:S(2)}, u32[]{:S(2)}) collective-permute-start(f32[2,32,1280]{2,1,0:T(8,128)S(1)} %get-tuple-element.12), channel_id=1, source_target_pairs={{0,6},{2,0},{4,2},{6,4},{1,7},{3,1},{5,3},{7,5},{8,14},{10,8},{12,... | collective-permute-start | bytes 983048 | tf_op jit(solution)/shard_map/ppermute | solution.py:362
  6.4 19.8 %collective-permute-start.2 = (f32[2,32,1280]{2,1,0:T(8,128)S(1)}, f32[2,32,1280]{2,1,0:T(8,128)S(1)}, u32[]{:S(2)}, u32[]{:S(2)}) collective-permute-start(f32[2,32,1280]{2,1,0:T(8,128)S(1)} %get-tuple-element.13), channel_id=1, source_target_pairs={{0,6},{2,0},{4,2},{6,4},{1,7},{3,1},{5,3},{7,5},{8,14},{10,8},{12,... | collective-permute-start | bytes 983048 | tf_op jit(solution)/shard_map/ppermute | solution.py:362
  7.8 18.4 %collective-permute-start.3 = (f32[2,32,1280]{2,1,0:T(8,128)S(1)}, f32[2,32,1280]{2,1,0:T(8,128)S(1)}, u32[]{:S(2)}, u32[]{:S(2)}) collective-permute-start(f32[2,32,1280]{2,1,0:T(8,128)S(1)} %get-tuple-element.11), channel_id=1, source_target_pairs={{0,2},{2,4},{4,6},{6,0},{1,3},{3,5},{5,7},{7,1},{8,10},{10,12},{12... | collective-permute-start | bytes 983048 | tf_op jit(solution)/shard_map/ppermute | solution.py:362
  13.6 0.7 copy-start.9
  16.2 11.0 %collective-permute-start.1 = (f32[2,32,1280]{2,1,0:T(8,128)}, f32[2,32,1280]{2,1,0:T(8,128)S(1)}, u32[]{:S(2)}, u32[]{:S(2)}) collective-permute-start(f32[2,32,1280]{2,1,0:T(8,128)} %added.2), channel_id=1, source_target_pairs={{0,2},{2,4},{4,6},{6,0},{1,3},{3,5},{5,7},{7,1},{8,10},{10,12},{12... | collective-permute-start | bytes 983048 | tf_op jit(solution)/shard_map/ppermute | solution.py:362
  16.2 0.7 copy-start.8
  18.7 8.4 %collective-permute-start.5 = (f32[2,32,1280]{2,1,0:T(8,128)}, f32[2,32,1280]{2,1,0:T(8,128)}, u32[]{:S(2)}, u32[]{:S(2)}) collective-permute-start(f32[2,32,1280]{2,1,0:T(8,128)} %added.3), channel_id=1, source_target_pairs={{0,6},{2,0},{4,2},{6,4},{1,7},{3,1},{5,3},{7,5},{8,14},{10,8},{12,... | collective-permute-start | bytes 983048 | tf_op jit(solution)/shard_map/ppermute | solution.py:362
  22.6 28.2 %copy-start = (bf16[256,512]{1,0:T(8,128)(2,1)S(1)}, bf16[256,512]{1,0:T(8,128)(2,1)}, u32[]{:S(2)}) copy-start(bf16[256,512]{1,0:T(8,128)(2,1)} %constant.73.clone.refs_7_.forth_ref) | copy-start | bytes 786436
  22.6 28.2 %copy-start.5 = (f32[2,32,128]{2,1,0:T(8,128)S(1)}, f32[2,32,128]{2,1,0:T(8,128)}, u32[]{:S(2)}) copy-start(f32[2,32,128]{2,1,0:T(8,128)} %constant.72.clone.refs_6_.turn_ref) | copy-start | bytes 98308
  22.6 18.4 %collective-permute-start.7 = (f32[4,32,1536]{2,1,0:T(8,128)S(1)}, f32[4,32,1536]{2,1,0:T(8,128)S(1)}, u32[]{:S(2)}, u32[]{:S(2)}) collective-permute-start(f32[4,32,1536]{2,1,0:T(8,128)S(1)} %fusion.2), channel_id=1, source_target_pairs={{0,1},{1,0},{2,3},{3,2},{4,5},{5,4},{6,7},{7,6},{8,9},{9,8},{10,11... | collective-permute-start | bytes 2359304 | tf_op jit(solution)/shard_map/ppermute | solution.py:366
  28.5 19.5 %collective-permute-start.6 = (f32[32,2560]{1,0:T(8,128)S(1)}, f32[32,2560]{1,0:T(8,128)S(1)}, u32[]{:S(2)}, u32[]{:S(2)}) collective-permute-start(f32[32,2560]{1,0:T(8,128)S(1)} %get-tuple-element.19), channel_id=1, source_target_pairs={{0,1},{1,0},{2,3},{3,2},{4,5},{5,4},{6,7},{7,6},{8,9},{9,8},{10,11... | collective-permute-start | bytes 983048 | tf_op jit(solution)/shard_map/ppermute | solution.py:366
  41.0 27.6 %copy-start.7 = (s32[4096,32]{0,1:T(8,128)S(1)}, s32[4096,32]{0,1:T(8,128)}, u32[]{:S(2)}) copy-start(s32[4096,32]{0,1:T(8,128)} %param.12) | copy-start | bytes 1572868
  42.4 6.4 %collective-permute-start.10 = (f32[32,1536]{1,0:T(8,128)S(1)}, f32[32,1536]{1,0:T(8,128)S(1)}, u32[]{:S(2)}, u32[]{:S(2)}) collective-permute-start(f32[32,1536]{1,0:T(8,128)S(1)} %get-tuple-element.15), channel_id=1, source_target_pairs={{0,4},{2,6},{4,0},{6,2},{1,5},{3,7},{5,1},{7,3},{8,12},{10,14},{12... | collective-permute-start | bytes 589832 | tf_op jit(solution)/shard_map/ppermute | solution.py:362
  42.7 8.1 %collective-permute-start.8 = (f32[32,1536]{1,0:T(8,128)S(1)}, f32[32,1536]{1,0:T(8,128)S(1)}, u32[]{:S(2)}, u32[]{:S(2)}) collective-permute-start(f32[32,1536]{1,0:T(8,128)S(1)} %get-tuple-element.17), channel_id=1, source_target_pairs={{0,2},{2,4},{4,6},{6,0},{1,3},{3,5},{5,7},{7,1},{8,10},{10,12},{12... | collective-permute-start | bytes 589832 | tf_op jit(solution)/shard_map/ppermute | solution.py:362
  43.1 7.7 %collective-permute-start.9 = (f32[32,1536]{1,0:T(8,128)S(1)}, f32[32,1536]{1,0:T(8,128)S(1)}, u32[]{:S(2)}, u32[]{:S(2)}) collective-permute-start(f32[32,1536]{1,0:T(8,128)S(1)} %get-tuple-element.16), channel_id=1, source_target_pairs={{0,6},{2,0},{4,2},{6,4},{1,7},{3,1},{5,3},{7,5},{8,14},{10,8},{12,... | collective-permute-start | bytes 589832 | tf_op jit(solution)/shard_map/ppermute | solution.py:362
  50.8 37.2 %copy-start.1 = (bf16[256,512]{1,0:T(8,128)(2,1)S(1)}, bf16[256,512]{1,0:T(8,128)(2,1)}, u32[]{:S(2)}) copy-start(bf16[256,512]{1,0:T(8,128)(2,1)} %constant.75.clone.back_ref) | copy-start | bytes 786436
  50.8 37.2 %copy-start.2 = (bf16[512,256]{1,0:T(8,128)(2,1)S(1)}, bf16[512,256]{1,0:T(8,128)(2,1)}, u32[]{:S(2)}) copy-start(bf16[512,256]{1,0:T(8,128)(2,1)} %constant.76.clone.short_forth_ref) | copy-start | bytes 786436
  50.9 37.2 %copy-start.3 = (bf16[512,256]{1,0:T(8,128)(2,1)S(1)}, bf16[512,256]{1,0:T(8,128)(2,1)}, u32[]{:S(2)}) copy-start(bf16[512,256]{1,0:T(8,128)(2,1)} %constant.77.clone.short_back_ref) | copy-start | bytes 786436
  50.9 37.2 %copy-start.6 = (f32[2,128,128]{2,1,0:T(8,128)S(1)}, f32[2,128,128]{2,1,0:T(8,128)}, u32[]{:S(2)}) copy-start(f32[2,128,128]{2,1,0:T(8,128)} %constant.74.clone.turn_ref) | copy-start | bytes 393220
  52.9 35.2 %all-to-all-start = ((f32[128,1,2048]{2,1,0:T(1,128)}), f32[128,1,2048]{2,1,0:T(1,128)S(1)}, u32[]{:S(2)}, u32[]{:S(2)}) async-start(f32[128,1,2048]{2,1,0:T(1,128)} %bitcast.20), calls=%async_computation | async-start | bytes 2097152 | tf_op jit(solution)/shard_map/all_to_all | solution.py:357
  69.0 50.2 %copy-start.4 = (bf16[512,256]{1,0:T(8,128)(2,1)S(1)}, bf16[512,256]{1,0:T(8,128)(2,1)}, u32[]{:S(2)}) copy-start(bf16[512,256]{1,0:T(8,128)(2,1)} %constant.78.clone.table_ref) | copy-start | bytes 786436

commit v2 on v1

--- a/solution.py
+++ b/solution.py
@@ -17,7 +17,7 @@
 ROWS = ("rows_0", "rows_1", "rows_2")
 PLANES = ("planes_0", "planes_1")
 ROWS_PLANES = ROWS + PLANES
-FORTH = 16
+FORTH = 9
 BACK = 17
 EARLY_HALF = 1280
 EARLY = 2 * EARLY_HALF
@@ -175,11 +175,7 @@
             for term in terms[1:]:
                 total = total + term[rows, lanes]
             pieces.append(total)
-        half = transformed_real(pieces)
-        for k in range(SHORT):
-            real, imag = half[k] if k <= SHORT // 2 else half[SHORT - k]
-            if k > SHORT // 2:
-                imag = None if imag is None else -imag
+        for k, (real, imag) in enumerate(transformed_real(pieces)):
             cosine = turn_ref[0, k : k + 1, :]
             sine = turn_ref[1, k : k + 1, :]
             if imag is None:
@@ -188,15 +184,21 @@
             else:
                 held_ref[k, block, :, :LONG] = real * cosine + imag * sine
                 held_ref[k, block, :, LONG:] = imag * cosine - real * sine
-    for quarter in range(4):
-        rows = held_ref[8 * quarter : 8 * quarter + 8].reshape(256, 2 * LONG)
+    for half in range(2):
+        rows = held_ref[8 * half : 8 * half + 8].reshape(256, 2 * LONG)
         spread = table_times_rows(forth_ref, rows)
         for part in range(2):
             for side in range(2):
-                tile = 8 * part + 2 * quarter + side
+                tile = 4 * part + 2 * half + side
                 out_ref[pl.ds(tile, LONG, FORTH), :] = spread[
                     LONG * part : LONG * part + LONG, LONG * side : LONG * side + LONG
                 ]
+    last = held_ref[SHORT // 2].reshape(SHORT, 2 * LONG)
+    real, imag = last[:, :LONG], last[:, LONG:]
+    turned = jnp.concatenate([imag, -real], axis=1)
+    nothing = jnp.zeros((2 * SHORT, 2 * LONG), jnp.float32)
+    spread = table_times_rows(forth_ref, jnp.concatenate([last, turned, nothing], axis=0))
+    out_ref[pl.ds(8, LONG, FORTH), :] = spread[:LONG]
 
 
 def part_terms(refs, column):
@@ -209,6 +211,8 @@
     first_ref,
     arrived_ref,
     bins_ref,
+    mirror_ref,
+    middle_ref,
     turn_ref,
     forth_ref,
     back_ref,
@@ -224,55 +228,41 @@
     height = ((height + N // 2) % N - N // 2).astype(jnp.float32)
     height_square = height * height
     first = first_ref[0]
-    for pair in range(4):
-        columns = []
-        for side in range(2):
-            group = 2 * pair + side
-            columns.append(
-                jnp.concatenate(
-                    [
-                        arrived_ref[pl.ds(group, LONG, FORTH), :],
-                        arrived_ref[pl.ds(8 + group, LONG, FORTH), :],
-                    ],
-                    axis=0,
-                )
-            )
-        spread = table_times(forth_ref, jnp.concatenate(columns, axis=1))
-        cosine = turn_ref[0]
-        sine = turn_ref[1]
+    cosine = turn_ref[0]
+    sine = turn_ref[1]
+    lone = lane < SHORT
+    edge = height == -(N // 2)
+
+    def forth(tiles):
+        spread = table_times(
+            forth_ref, jnp.concatenate([jnp.concatenate(tile, axis=0) for tile in tiles], axis=1)
+        )
         turned = []
-        for side in range(2):
+        for side in range(len(tiles)):
             lanes = slice(LONG * side, LONG * side + LONG)
             real, imag = spread[:LONG, lanes], spread[LONG:, lanes]
             turned.append(
                 jnp.concatenate([real * cosine + imag * sine, imag * cosine - real * sine], axis=1)
             )
         held = times_table(jnp.concatenate(turned, axis=0), short_forth_ref)
-        hats = []
-        for side in range(2):
-            group = 2 * pair + side
-            real = held[LONG * side : LONG * side + LONG, :LONG]
-            imag = held[LONG * side : LONG * side + LONG, LONG:]
-            across = first + 4 * group + lane // SHORT
-            across = ((across + N // 2) % N - N // 2).astype(jnp.float32)
-            across_square = across * across
-            square_norm = height_square + across_square
-            anchor = square_norm == 0.0
-            real = jnp.where(anchor, 0.0, real)
-            imag = jnp.where(anchor, 0.0, imag)
-            power_ref[LONG * group : LONG * group + LONG, :] = real * real + imag * imag
-            inverse = (1.0 / float(N) ** 2) / jnp.where(anchor, 1.0, square_norm)
-            kernel_real = (across_square - height_square) * inverse
-            kernel_imag = (across * height) * (2.0 * inverse)
-            hats.append(
-                jnp.concatenate(
-                    [
-                        kernel_real * real - kernel_imag * imag,
-                        kernel_real * imag + kernel_imag * real,
-                    ],
-                    axis=1,
-                )
-            )
+        rows = [slice(LONG * side, LONG * side + LONG) for side in range(len(tiles))]
+        return [(held[r, :LONG], held[r, LONG:]) for r in rows]
+
+    def kernels(group, pair):
+        real, imag = pair
+        across = first + 4 * group + lane // SHORT
+        across = ((across + N // 2) % N - N // 2).astype(jnp.float32)
+        across_square = across * across
+        square_norm = height_square + across_square
+        anchor = square_norm == 0.0
+        real = jnp.where(anchor, 0.0, real)
+        imag = jnp.where(anchor, 0.0, imag)
+        inverse = (1.0 / float(N) ** 2) / jnp.where(anchor, 1.0, square_norm)
+        kernel_real = (across_square - height_square) * inverse
+        kernel_imag = (across * height) * (2.0 * inverse)
+        return real, imag, kernel_real, kernel_imag
+
+    def back(hats):
         returned = times_table(jnp.concatenate(hats, axis=0), short_back_ref)
         columns = []
         for side in range(2):
@@ -281,25 +271,70 @@
             columns.append(
                 jnp.concatenate([real * cosine - imag * sine, imag * cosine + real * sine], axis=0)
             )
-        restored = table_times(back_ref, jnp.concatenate(columns, axis=1))
-        for part in range(2):
-            for side in range(2):
-                tile = 8 * part + 2 * pair + side
-                out_ref[pl.ds(tile, LONG, BACK), :] = restored[
-                    LONG * part : LONG * part + LONG, LONG * side : LONG * side + LONG
-                ]
-
-    def one_block(block, carry):
-        start = pl.multiple_of(block * 64, 64)
-        power = power_ref[pl.ds(start, 64), :]
-        bins = bins_ref[pl.ds(start, 64), :]
-        for band in range(NBINS):
-            chosen = jnp.where(bins == band, power, 0.0)
-            bands_ref[8 * band : 8 * band + 8, :] += jnp.sum(chosen.reshape(8, 8, LONG), axis=0)
-        return carry
+        return table_times(back_ref, jnp.concatenate(columns, axis=1))
+
+    middle = arrived_ref[pl.ds(8, LONG, FORTH), :]
+    tile = (jnp.where(lone, middle, 0.0), jnp.where(lone, pltpu.roll(middle, 96, 1), 0.0))
+    real, imag, kernel_real, kernel_imag = kernels(4, forth([tile])[0])
+    middle_power = real * real + imag * imag
+    middle_hat = (kernel_real * real - kernel_imag * imag, kernel_real * imag + kernel_imag * real)
+    for pair in range(2):
+        tiles = [
+            (arrived_ref[pl.ds(g, LONG, FORTH), :], arrived_ref[pl.ds(4 + g, LONG, FORTH), :])
+            for g in (2 * pair, 2 * pair + 1)
+        ]
+        hats_a, hats_b = [], []
+        for side, got in enumerate(forth(tiles)):
+            group = 2 * pair + side
+            real, imag, kernel_real, kernel_imag = kernels(group, got)
+            power = real * real + imag * imag
+            single = edge | lone if group == 0 else edge
+            odd = jnp.where(single, kernel_imag, 0.0)
+            even = jnp.where(single, 0.0, kernel_imag)
+            b_real, b_imag = even * real, even * imag
+            mirror_power = power
+            if group == 0:
+                b_real = jnp.where(lone, middle_hat[0], b_real)
+                b_imag = jnp.where(lone, middle_hat[1], b_imag)
+                mirror_power = jnp.where(lone, middle_power, power)
+            power_ref[LONG * group : LONG * group + LONG, :] = power
+            power_ref[LONG * (4 + group) : LONG * (5 + group), :] = mirror_power
+            hats_a.append(
+                jnp.concatenate(
+                    [kernel_real * real - odd * imag, kernel_real * imag + odd * real], axis=1
+                )
+            )
+            hats_b.append(jnp.concatenate([b_real, b_imag], axis=1))
+        for which, hats in enumerate((hats_a, hats_b)):
+            restored = back(hats)
+            for part in range(2):
+                for side in range(2):
+                    tile = 8 * part + 4 * which + 2 * pair + side
+                    out_ref[pl.ds(tile, LONG, BACK), :] = restored[
+                        LONG * part : LONG * part + LONG, LONG * side : LONG * side + LONG
+                    ]
+
+    def counted(tile_ref, offset, inner=None):
+        def one_block(block, carry):
+            start = pl.multiple_of(block * 64, 64)
+            power = power_ref[pl.ds(offset + start, 64), :]
+            bins = tile_ref[pl.ds(start, 64), :]
+            if inner is not None:
+                row = jnp.minimum(start, LONG - 64)
+                here = (lane[:64] < SHORT) & (start < LONG)
+                bins = jnp.where(here, inner[pl.ds(pl.multiple_of(row, 64), 64), :], bins)
+            for band in range(NBINS):
+                chosen = jnp.where(bins == band, power, 0.0)
+                bands_ref[8 * band : 8 * band + 8, :] += jnp.sum(
+                    chosen.reshape(8, 8, LONG), axis=0
+                )
+            return carry
+
+        lax.fori_loop(0, 4 * LONG // 64, one_block, 0)
 
     bands_ref[...] = jnp.zeros_like(bands_ref)
-    lax.fori_loop(0, 8 * LONG // 64, one_block, 0)
+    counted(bins_ref, 0)
+    counted(mirror_ref, 4 * LONG, middle_ref)
     sums = jnp.sum(bands_ref[...].reshape(NBINS, 8, LONG), axis=1)
     sums = jnp.concatenate([sums, jnp.zeros((LONG - NBINS, LONG), jnp.float32)], axis=0)
     line = jnp.sum(sums.T, axis=0, keepdims=True) * (NBINS / float(N) ** 4)
@@ -321,13 +356,23 @@
     bands = jnp.sum(arrived_ref[pl.ds(16, LONG, BACK), :], axis=0, keepdims=True)
     spectrum_ref[...] = bands[:, :NBINS]
     for block in range(4):
-        pieces = []
-        for k in range(SHORT):
-            rows = slice(SHORT * k + 8 * block, SHORT * k + 8 * block + 8)
-            cosine = turn_ref[0, k : k + 1, :]
-            sine = turn_ref[1, k : k + 1, :]
-            real, imag = held_ref[rows, :LONG], held_ref[rows, LONG:]
-            pieces.append((real * cosine - imag * sine, imag * cosine + real * sine))
+        pieces = [None] * SHORT
+        for k in range(SHORT // 2):
+            turned = []
+            for which in range(2):
+                start = SHORT * (SHORT // 2 * which + k) + 8 * block
+                rows = slice(start, start + 8)
+                turn = k + SHORT // 2 if which and not k else k
+                cosine = turn_ref[0, turn : turn + 1, :]
+                sine = turn_ref[1, turn : turn + 1, :]
+                real, imag = held_ref[rows, :LONG], held_ref[rows, LONG:]
+                turned.append((real * cosine - imag * sine, imag * cosine + real * sine))
+            (a_real, a_imag), (b_real, b_imag) = turned
+            if k == 0:
+                pieces[0], pieces[SHORT // 2] = turned
+            else:
+                pieces[k] = (a_real - b_imag, a_imag + b_real)
+                pieces[SHORT - k] = (a_real + b_imag, b_real - a_imag)
         for n, (real, imag) in enumerate(transformed(pieces, 1.0)):
             real_ref[8 * block : 8 * block + 8, LONG * n : LONG * n + LONG] = real
             imag_ref[8 * block : 8 * block + 8, LONG * n : LONG * n + LONG] = imag
@@ -366,42 +411,8 @@
     return lax.ppermute(array, PLANES[1], [(0, 1), (1, 0)])
 
 
-def apart(array):
-    return lax.optimization_barrier(array)
-
-
-def added_kernel(index_ref, scale_ref, own_ref, far_ref, out_ref):
-    out_ref[...] = own_ref[0] * scale_ref[0] + far_ref[...]
-
-
-def added(index, scale, whole, side, far):
-    shape = (1,) + far.shape
-    lead = (0,) * (len(shape) - 2)
-    here = lambda i, index_ref: (index_ref[0],) + lead + (side,)
-    rest = lambda i, index_ref: lead + (0,)
-    grid_spec = pltpu.PrefetchScalarGridSpec(
-        num_scalar_prefetch=1,
-        grid=(1,),
-        in_specs=[
-            pl.BlockSpec(memory_space=pltpu.SMEM),
-            pl.BlockSpec(shape, here),
-            pl.BlockSpec(far.shape, rest),
-        ],
-        out_specs=pl.BlockSpec(far.shape, rest),
-    )
-    return pl.pallas_call(
-        added_kernel, grid_spec=grid_spec, out_shape=f32(*far.shape), name="added"
-    )(index.reshape(1), scale.reshape(1), whole, far)
-
-
-def summed_along(piece, bound):
-    far_up = along(piece(2, 0), 1)
-    far_down = along(piece(2, 1), -1)
-    up_free = along(piece(1, 1), 1)
-    down_free = along(piece(-1, 0), -1)
-    up_bound = along(bound(1, 0, far_up), 1)
-    down_bound = along(bound(-1, 1, far_down), -1)
-    return (up_bound, down_free), (up_free, down_bound)
+def after(array, other):
+    return lax.optimization_barrier((array, other))[0]
 
 
 def plane_sum(density, weight):
@@ -411,42 +422,63 @@
     blocks = density.reshape(4, 2, -1, length)
     rows = blocks.shape[2]
 
-    def early(step, side):
+    def early(source, step, side):
         got = lax.dynamic_slice(
-            blocks, ((here + step) & 3, 0, 0, side * EARLY_HALF), (1, 2, rows, EARLY_HALF)
+            source, ((here + step) & 3, 0, 0, side * EARLY_HALF), (1, 2, rows, EARLY_HALF)
         )
         return got[0] * weight
 
-    def early_bound(step, side, far):
-        return added((here + step) & 3, weight, blocks, side, far)
-
-    def late_block(half):
-        got = lax.dynamic_slice(
-            blocks, (0, half, 0, EARLY), (4, 1, rows, length - EARLY)
-        )
+    def late_block(source, half):
+        got = lax.dynamic_slice(source, (0, half, 0, EARLY), (4, 1, rows, length - EARLY))
         return got[:, 0] * weight
 
-    late_other = swapped(late_block(1 - upper))
-    left, right = summed_along(early, early_bound)
-    late = apart(late_block(upper) + late_other)
+    far_up = along(early(blocks, 2, 0), 1)
+    far_down = along(early(blocks, 2, 1), -1)
+    late_sent = late_block(blocks, 1 - upper)
+    late_other = swapped(late_sent)
+    up_free = along(early(blocks, 1, 1), 1)
+    down_free = along(early(blocks, -1, 0), -1)
+    up_bound = along(early(after(blocks, far_up), 1, 0) + far_up, 1)
+    down_bound = along(early(after(blocks, far_down), -1, 1) + far_down, -1)
+    late = late_block(after(blocks, late_other), upper) + late_other
 
     def late_piece(step):
         return lax.dynamic_index_in_dim(late, (here + step) & 3, 0, keepdims=False)
 
+    late_terms = [along(late_piece(step), step) for step in (1, -1, 2)]
+    whole = after(blocks, up_bound)
     early_sum = jnp.concatenate(
-        [early(0, 0) + left[0] + left[1], early(0, 1) + right[0] + right[1]], axis=-1
+        [
+            early(whole, 0, 0) + up_bound + down_free,
+            early(whole, 0, 1) + up_free + down_bound,
+        ],
+        axis=-1,
     )
+    sent = lax.dynamic_index_in_dim(early_sum, 1 - upper, 0, keepdims=False)
     mine = lax.dynamic_index_in_dim(early_sum, upper, 0, keepdims=False)
-    other = swapped(lax.dynamic_index_in_dim(early_sum, 1 - upper, 0, keepdims=False))
-    late_terms = [along(late_piece(step), step) for step in (1, -1, 2)]
+    other = swapped(sent)
     return (mine, other, late_piece(0), *late_terms)
+
+
+def tiled(columns):
+    return columns.reshape(4, 4, SHORT, LONG).transpose(0, 3, 1, 2).reshape(4 * LONG, LONG)
+
+
+def swapped_mirror(array):
+    return lax.ppermute(array, ROWS_PLANES, [(i, LONG - 1 - i) for i in range(LONG)])
 
 
 def on_device(density, lens_weight, spectrum_bin):
     held = tables()
     device = lax.axis_index(ROWS_PLANES)
     parts = plane_sum(density[0], lens_weight[0])
-    bins = spectrum_bin.reshape(SHORT, LONG, 8, 4).transpose(2, 1, 3, 0).reshape(8 * LONG, LONG)
+    columns = spectrum_bin.T
+    mirrored = jnp.roll(columns[SHORT // 2 + 1 :, ::-1], 1, axis=1)[::-1]
+    mirrored = tiled(jnp.concatenate([columns[:1], mirrored], axis=0))
+    bins = tiled(columns[: SHORT // 2])
+    middle = columns[SHORT // 2].reshape(SHORT, LONG).T
+    middle = jnp.pad(middle, ((0, 0), (0, 3 * SHORT)))
+    mirror = swapped_mirror(after(mirrored, parts[1]))
     sent = call(
         rows_forth_kernel,
         f32(LONG * FORTH, LONG),
@@ -462,6 +494,8 @@
             (device * SHORT).reshape(1),
             arrived,
             bins,
+            mirror,
+            middle,
             held["column_turn"],
             held["forth"],
             held["back"],

time: 121 us -> 120 us (level)
  waiting for transfers between devices: 38 us -> 28.2 us
  starting transfers between devices: 33.7 us -> 41.8 us
  Pallas kernels: 14.8 us -> 9.69 us
  other arithmetic: 5.19 us -> 9 us
    all_to_all x1, waiting for transfers between devices: 16.9 us -> 0.01 us  [exchanged(): lax.all_to_all(blocks, ROWS_PLANES, split_axis=0, concat_axis=0, tiled=True)]
    ppermute x0 -> x1, waiting for transfers between devices: none -> 10 us  [swapped_mirror(): lax.ppermute(array, ROWS_PLANES, [(i, LONG - 1 - i) for i in range(LONG)])]
    ppermute x0 -> x1, starting transfers between devices: none -> 8.05 us  [swapped_mirror(): lax.ppermute(array, ROWS_PLANES, [(i, LONG - 1 - i) for i in range(LONG)])]
    ppermute x2, waiting for transfers between devices: 11.6 us -> 6.44 us  [swapped(): return lax.ppermute(array, PLANES[1], [(0, 1), (1, 0)])]
    add x2 -> x4, other arithmetic: 2.55 us -> 6.21 us  [the longest x1 1.74 us: plane_sum(): up_bound = along(early(after(blocks, far_up), 1, 0) + far_up, 1)]
    pallas_call x2 -> x0, Pallas kernels: 3.65 us -> none  [added(): pl.pallas_call(added_kernel, grid_spec=grid_spec, out_shape=f32(*far.shap...]
    ppermute x9, waiting for transfers between devices: 9.53 us -> 11.7 us  [along(): lax.ppermute(array, PLANES[0], [(i, (i + step) % 4) for i in range(4)])]
    pallas_call x3, Pallas kernels: 11.1 us -> 9.69 us  [call(): pl.pallas_call(kernel, out_shape=outs, in_specs=specs, out_specs=jax.tree...]
  transfers between devices with their start and end apart: 12 -> 13, of which waited for: 7 -> 6; matrix products, arithmetic and copies ran while one was open for 5% -> 11% of each run, Pallas kernels for 3% -> 0%
where the time goes in v2:
time: 120 us
  starting transfers between devices  41.8 us (35%)
  waiting for transfers between devices  28.2 us (24%)
  blocking collectives  24.4 us (20%)
  Pallas kernels  9.69 us (8%)
  other arithmetic  9 us (8%)
  local copies, waits for them, and re-layouts  5.08 us (4%)
  between operations  1.54 us (1%)
    all_to_all x1, blocking collectives, exchanged(): lax.all_to_all(blocks, ROWS_PLANES, split_axis=0, concat_axis=0, tiled=True)  24.4 us
    all_to_all x1, starting transfers between devices, exchanged(): lax.all_to_all(blocks, ROWS_PLANES, split_axis=0, concat_axis=0, tiled=True)  15.8 us
    ppermute x9, waiting for transfers between devices, along(): lax.ppermute(array, PLANES[0], [(i, (i + step) % 4) for i in range(4)])  11.7 us
    ppermute x9, starting transfers between devices, along(): lax.ppermute(array, PLANES[0], [(i, (i + step) % 4) for i in range(4)])  10.8 us
    ppermute x1, waiting for transfers between devices, swapped_mirror(): lax.ppermute(array, ROWS_PLANES, [(i, LONG - 1 - i) for i in range(LONG)])  10 us
    pallas_call x3, Pallas kernels, call(): pl.pallas_call(kernel, out_shape=outs, in_specs=specs, out_specs=jax.tree...  9.69 us
    ppermute x1, starting transfers between devices, swapped_mirror(): lax.ppermute(array, ROWS_PLANES, [(i, LONG - 1 - i) for i in range(LONG)])  8.05 us
    ppermute x2, starting transfers between devices, swapped(): return lax.ppermute(array, PLANES[1], [(0, 1), (1, 0)])  7.12 us
  transfers between devices with their start and end apart: 13, of which 6 were waited for; matrix products, arithmetic and copies ran while one was open for 11% of the time, Pallas kernels for 0%

profile of v2, /device:TPU:1, one launch (start us, length us, event | category | flops | bytes accessed | tf_op | source)
XLA Modules:
  0.0 119.6 jit_solution(13312967943582423305)
XLA Ops:
  1.3 1.4 %multiply_bitcast_fusion.1 = (f32[2,32,1280]{2,1,0:T(8,128)S(1)}, f32[2,32,1280]{2,1,0:T(8,128)S(1)}, f32[2,32,1280]{2,1,0:T(8,128)S(1)}, f32[2,32,1280]{2,1,0:T(8,128)S(1)}) fusion(f32[4,2,32,4096]{3,2,1,0:T(8,128)} %bitcast.85, s32[]{:T(128)S(6)} %select_n.31, f32[]{:T(128)} %bitcast.81, s32[]{:T(128)S(6)} %select_n.30, s32[]{:T(128)S(6)} %select_n.33), kind=kLoop, calls=%fused_computation.18 | loop fusion | flops 327680 | bytes 2621456 | tf_op jit(solution)/shard_map/mul | solution.py:429
  2.7 2.2 %collective-permute-start = (f32[2,32,1280]{2,1,0:T(8,128)S(1)}, f32[2,32,1280]{2,1,0:T(8,128)S(1)}, u32[]{:S(2)}, u32[]{:S(2)}) collective-permute-start(f32[2,32,1280]{2,1,0:T(8,128)S(1)} %get-tuple-element.24), channel_id=1, source_target_pairs={{0,2},{2,4},{4,6},{6,0},{1,3},{3,5},{5,7},{7,1},{8,10},{10,12},{12... | collective-permute-start | bytes 983048 | tf_op jit(solution)/shard_map/ppermute | solution.py:407
  4.9 1.5 %collective-permute-start.4 = (f32[2,32,1280]{2,1,0:T(8,128)S(1)}, f32[2,32,1280]{2,1,0:T(8,128)S(1)}, u32[]{:S(2)}, u32[]{:S(2)}) collective-permute-start(f32[2,32,1280]{2,1,0:T(8,128)S(1)} %get-tuple-element.22), channel_id=1, source_target_pairs={{0,6},{2,0},{4,2},{6,4},{1,7},{3,1},{5,3},{7,5},{8,14},{10,8},{12,... | collective-permute-start | bytes 983048 | tf_op jit(solution)/shard_map/ppermute | solution.py:407
  6.4 1.4 %collective-permute-start.2 = (f32[2,32,1280]{2,1,0:T(8,128)S(1)}, f32[2,32,1280]{2,1,0:T(8,128)S(1)}, u32[]{:S(2)}, u32[]{:S(2)}) collective-permute-start(f32[2,32,1280]{2,1,0:T(8,128)S(1)} %get-tuple-element.23), channel_id=1, source_target_pairs={{0,6},{2,0},{4,2},{6,4},{1,7},{3,1},{5,3},{7,5},{8,14},{10,8},{12,... | collective-permute-start | bytes 983048 | tf_op jit(solution)/shard_map/ppermute | solution.py:407
  7.8 5.8 %collective-permute-done = f32[2,32,1280]{2,1,0:T(8,128)S(1)} collective-permute-done((f32[2,32,1280]{2,1,0:T(8,128)S(1)}, f32[2,32,1280]{2,1,0:T(8,128)S(1)}, u32[]{:S(2)}, u32[]{:S(2)}) %collective-permute-start) | collective-permute-done | bytes 327712 | tf_op jit(solution)/shard_map/ppermute | solution.py:407
  13.6 1.7 %bitcast_add_fusion.4 = f32[2,32,1280]{2,1,0:T(8,128)} fusion(f32[2,32,1280]{2,1,0:T(8,128)S(1)} %collective-permute-done, f32[4,2,32,4096]{3,2,1,0:T(8,128)} %bitcast.86, s32[]{:T(128)S(6)} %select_n.31, f32[]{:T(128)} %bitcast.80), kind=kLoop, calls=%fused_computation.16 | loop fusion | flops 163840 | bytes 983048 | tf_op jit(solution)/shard_map/add | solution.py:441
  15.4 1.7 %bitcast_add_fusion.1 = f32[2,32,1280]{2,1,0:T(8,128)} fusion(f32[2,32,1280]{2,1,0:T(8,128)S(1)} %collective-permute-done.4, f32[4,2,32,4096]{3,2,1,0:T(8,128)} %bitcast.87, s32[]{:T(128)S(6)} %select_n.33, f32[]{:T(128)} %bitcast.79), kind=kLoop, calls=%fused_computation.11 | loop fusion | flops 163840 | bytes 983048 | tf_op jit(solution)/shard_map/add | solution.py:442
  17.1 2.7 %collective-permute-start.5 = (f32[2,32,1280]{2,1,0:T(8,128)}, f32[2,32,1280]{2,1,0:T(8,128)}, u32[]{:S(2)}, u32[]{:S(2)}) collective-permute-start(f32[2,32,1280]{2,1,0:T(8,128)} %bitcast_add_fusion.1), channel_id=1, source_target_pairs={{0,6},{2,0},{4,2},{6,4},{1,7},{3,1},{5,3},{7,5},{8,14},{10,8},{12,... | collective-permute-start | bytes 983048 | tf_op jit(solution)/shard_map/ppermute | solution.py:407
  19.8 1.2 %fusion = f32[4,32,1536]{2,1,0:T(8,128)S(1)} fusion(f32[4,2,32,4096]{3,2,1,0:T(8,128)} %bitcast.88, s32[]{:T(128)S(6)} %select_n.35, f32[]{:T(128)} %bitcast.77), kind=kLoop, calls=%fused_computation.1 | loop fusion | flops 196608 | bytes 1572872 | tf_op jit(solution)/shard_map/mul | solution.py:433
  21.0 3.6 %collective-permute-start.7 = (f32[4,32,1536]{2,1,0:T(8,128)S(1)}, f32[4,32,1536]{2,1,0:T(8,128)S(1)}, u32[]{:S(2)}, u32[]{:S(2)}) collective-permute-start(f32[4,32,1536]{2,1,0:T(8,128)S(1)} %fusion), channel_id=1, source_target_pairs={{0,1},{1,0},{2,3},{3,2},{4,5},{5,4},{6,7},{7,6},{8,9},{9,8},{10,11... | collective-permute-start | bytes 2359304 | tf_op jit(solution)/shard_map/ppermute | solution.py:411
  24.5 3.2 %collective-permute-done.1 = f32[2,32,1280]{2,1,0:T(8,128)} collective-permute-done((f32[2,32,1280]{2,1,0:T(8,128)}, f32[2,32,1280]{2,1,0:T(8,128)}, u32[]{:S(2)}, u32[]{:S(2)}) %collective-permute-start.1) | collective-permute-done | bytes 327712 | tf_op jit(solution)/shard_map/ppermute | solution.py:407
  27.8 1.5 %fusion.5 = (f32[2,32,1280]{2,1,0:T(8,128)S(1)}, f32[2,32,1280]{2,1,0:T(8,128)S(1)}) fusion(f32[2,32,1280]{2,1,0:T(8,128)} %collective-permute-done.5, f32[2,32,1280]{2,1,0:T(8,128)} %collective-permute-done.3, f32[4,2,32,4096]{3,2,1,0:T(8,128)} %bitcast.89, s32[]{:T(128)S(6)} %select_n.32, f32[]{:T(128)} %bitcast.76, ...), kind=kLoop, calls=%fused_computation.13 | loop fusion | flops 491520 | bytes 2621448 | tf_op jit(solution)/shard_map/add | solution.py:453
  29.4 3.6 %collective-permute-start.6 = (f32[32,2560]{1,0:T(8,128)S(1)}, f32[32,2560]{1,0:T(8,128)S(1)}, u32[]{:S(2)}, u32[]{:S(2)}) collective-permute-start(f32[32,2560]{1,0:T(8,128)S(1)} %get-tuple-element.29), channel_id=1, source_target_pairs={{0,1},{1,0},{2,3},{3,2},{4,5},{5,4},{6,7},{7,6},{8,9},{9,8},{10,11... | collective-permute-start | bytes 983048 | tf_op jit(solution)/shard_map/ppermute | solution.py:411
  32.9 6.4 %collective-permute-done.7 = f32[4,32,1536]{2,1,0:T(8,128)S(1)} collective-permute-done((f32[4,32,1536]{2,1,0:T(8,128)S(1)}, f32[4,32,1536]{2,1,0:T(8,128)S(1)}, u32[]{:S(2)}, u32[]{:S(2)}) %collective-permute-start.7) | collective-permute-done | bytes 786464 | tf_op jit(solution)/shard_map/ppermute | solution.py:411
  39.4 1.2 %bitcast_add_fusion = f32[4,32,1536]{2,1,0:T(8,128)S(1)} fusion(f32[4,32,1536]{2,1,0:T(8,128)S(1)} %collective-permute-done.7, s32[]{:T(128)S(6)} %select_n.34, f32[]{:T(128)} %bitcast.78, f32[4,2,32,4096]{3,2,1,0:T(8,128)} %bitcast.90), kind=kLoop, calls=%fused_computation.2 | loop fusion | flops 393216 | bytes 2359812 | tf_op jit(solution)/shard_map/add | solution.py:443
  40.6 0.8 dynamic-slice_bitcast_fusion
  41.4 0.2 collective-permute-start.10
  41.7 0.4 collective-permute-start.8
  42.1 2.3 %collective-permute-start.9 = (f32[32,1536]{1,0:T(8,128)S(1)}, f32[32,1536]{1,0:T(8,128)S(1)}, u32[]{:S(2)}, u32[]{:S(2)}) collective-permute-start(f32[32,1536]{1,0:T(8,128)S(1)} %get-tuple-element.26), channel_id=1, source_target_pairs={{0,6},{2,0},{4,2},{6,4},{1,7},{3,1},{5,3},{7,5},{8,14},{10,8},{12,... | collective-permute-start | bytes 589832 | tf_op jit(solution)/shard_map/ppermute | solution.py:407
  44.5 2.3 %reverse.2 = s32[15,4096]{1,0:T(8,128)S(1)} reverse(s32[15,4096]{1,0:T(8,128)S(1)} %bitcast.91), dimensions={1} | reverse | bytes 491520
  46.8 0.2 slice.36
  47.0 1.0 collective-permute-done.10.refs_5_
  48.0 1.7 %collective-permute-done.8.refs_3_ = f32[32,1536]{1,0:T(8,128)S(1)} collective-permute-done((f32[32,1536]{1,0:T(8,128)}, f32[32,1536]{1,0:T(8,128)S(1)}, u32[]{:S(2)}, u32[]{:S(2)}) %collective-permute-start.8) | collective-permute-done | bytes 196640 | tf_op jit(solution)/shard_map/ppermute | solution.py:407
  49.7 1.5 %shard_map.121 = f32[1152,128]{1,0:T(8,128)} custom-call(f32[32,2560]{1,0:T(8,128)S(1)} %get-tuple-element.30.refs_0_, f32[32,2560]{1,0:T(8,128)S(1)} %collective-permute-done.6.refs_1_, f32[32,1536]{1,0:T(8,128)S(1)} %get-tuple-element.28.refs_2_, f32[32,1536]{1,0:T(8,128)S(1)} %collective-permute-done.8.refs_3_, ...), custom_call_target="tpu_custom_call" | custom-call | tf_op jit(solution)/shard_map/pallas_call | solution.py:386
  51.2 15.8 %all-to-all-start = ((f32[128,1,1152]{2,1,0:T(1,128)}), f32[128,1,1152]{2,1,0:T(1,128)S(1)}, u32[]{:S(2)}, u32[]{:S(2)}) async-start(f32[128,1,1152]{2,1,0:T(1,128)} %bitcast.19), calls=%async_computation | async-start | bytes 1179648 | tf_op jit(solution)/shard_map/all_to_all | solution.py:402
  67.2 0.8 rev.4
  68.1 0.2 copy.28
  68.4 8.1 %collective-permute-start.11 = (s32[512,128]{1,0:T(8,128)S(1)}, s32[512,128]{1,0:T(8,128)S(1)}, u32[]{:S(2)}, u32[]{:S(2)}) collective-permute-start(s32[512,128]{1,0:T(8,128)S(1)} %copy.29), channel_id=1, source_target_pairs={{0,127},{1,126},{2,125},{3,124},{4,123},{5,122},{6,121},{7,120},{8... | collective-permute-start | bytes 786440 | tf_op jit(solution)/shard_map/ppermute | solution.py:468
  77.0 10.0 %collective-permute-done.11.mirror_ref = s32[512,128]{1,0:T(8,128)S(1)} collective-permute-done((s32[512,128]{1,0:T(8,128)S(1)}, s32[512,128]{1,0:T(8,128)S(1)}, u32[]{:S(2)}, u32[]{:S(2)}) %collective-permute-start.11) | collective-permute-done | bytes 262176 | tf_op jit(solution)/shard_map/ppermute | solution.py:468
  87.0 6.3 %shard_map.122 = f32[2176,128]{1,0:T(8,128)S(1)} custom-call(s32[1]{0:T(128)} %bitcast.first_ref, f32[1152,128]{1,0:T(8,128)S(1)} %bitcast.84, s32[512,128]{1,0:T(8,128)S(1)} %copy.31.bins_ref, s32[512,128]{1,0:T(8,128)S(1)} %collective-permute-done.11.mirror_ref, s32[128,128]{1,0:T(8,128)S(1)} %pad.4.middle_ref, f32[2,128,128]{2,1,0:T(8,128)S(1)} %copy-done.6, ...), custom_call_target="tpu_custom_call" | custom-call | tf_op jit(solution)/shard_map/pallas_call | solution.py:386
  93.3 24.4 %all_to_all.10 = f32[128,1,2176]{2,1,0:T(1,128)S(1)} all-to-all(f32[128,1,2176]{2,1,0:T(1,128)S(1)} %bitcast.83), channel_id=1, replica_groups=mesh['rows_0'=4,'rows_1'=2,'rows_2'=2,'planes_0'=4,'planes_1'=2] {'rows_..., dimensions={0} | all-to-all | bytes 2228224 | tf_op jit(solution)/shard_map/all_to_all | solution.py:402
  117.8 1.9 %shard_map.123 = (f32[32,4096]{1,0:T(8,128)}, f32[32,4096]{1,0:T(8,128)}, f32[1,64]{1,0:T(1,128)}) custom-call(f32[2176,128]{1,0:T(8,128)S(1)} %bitcast.82, f32[2,32,128]{2,1,0:T(8,128)S(1)} %copy-done.5, bf16[512,256]{1,0:T(8,128)(2,1)S(1)} %copy-done.4), custom_call_target="tpu_custom_call" | custom-call | tf_op jit(solution)/shard_map/pallas_call | solution.py:386
  (41 shorter events, 1.2 us)
Async XLA Ops:
  2.7 10.9 %collective-permute-start = (f32[2,32,1280]{2,1,0:T(8,128)S(1)}, f32[2,32,1280]{2,1,0:T(8,128)S(1)}, u32[]{:S(2)}, u32[]{:S(2)}) collective-permute-start(f32[2,32,1280]{2,1,0:T(8,128)S(1)} %get-tuple-element.24), channel_id=1, source_target_pairs={{0,2},{2,4},{4,6},{6,0},{1,3},{3,5},{5,7},{7,1},{8,10},{10,12},{12... | collective-permute-start | bytes 983048 | tf_op jit(solution)/shard_map/ppermute | solution.py:407
  4.9 10.5 %collective-permute-start.4 = (f32[2,32,1280]{2,1,0:T(8,128)S(1)}, f32[2,32,1280]{2,1,0:T(8,128)S(1)}, u32[]{:S(2)}, u32[]{:S(2)}) collective-permute-start(f32[2,32,1280]{2,1,0:T(8,128)S(1)} %get-tuple-element.22), channel_id=1, source_target_pairs={{0,6},{2,0},{4,2},{6,4},{1,7},{3,1},{5,3},{7,5},{8,14},{10,8},{12,... | collective-permute-start | bytes 983048 | tf_op jit(solution)/shard_map/ppermute | solution.py:407
  6.4 21.4 %collective-permute-start.2 = (f32[2,32,1280]{2,1,0:T(8,128)S(1)}, f32[2,32,1280]{2,1,0:T(8,128)S(1)}, u32[]{:S(2)}, u32[]{:S(2)}) collective-permute-start(f32[2,32,1280]{2,1,0:T(8,128)S(1)} %get-tuple-element.23), channel_id=1, source_target_pairs={{0,6},{2,0},{4,2},{6,4},{1,7},{3,1},{5,3},{7,5},{8,14},{10,8},{12,... | collective-permute-start | bytes 983048 | tf_op jit(solution)/shard_map/ppermute | solution.py:407
  7.8 20.0 %collective-permute-start.3 = (f32[2,32,1280]{2,1,0:T(8,128)S(1)}, f32[2,32,1280]{2,1,0:T(8,128)}, u32[]{:S(2)}, u32[]{:S(2)}) collective-permute-start(f32[2,32,1280]{2,1,0:T(8,128)S(1)} %get-tuple-element.21), channel_id=1, source_target_pairs={{0,2},{2,4},{4,6},{6,0},{1,3},{3,5},{5,7},{7,1},{8,10},{10,12},{12... | collective-permute-start | bytes 983048 | tf_op jit(solution)/shard_map/ppermute | solution.py:407
  15.3 12.4 %collective-permute-start.1 = (f32[2,32,1280]{2,1,0:T(8,128)}, f32[2,32,1280]{2,1,0:T(8,128)}, u32[]{:S(2)}, u32[]{:S(2)}) collective-permute-start(f32[2,32,1280]{2,1,0:T(8,128)} %bitcast_add_fusion.4), channel_id=1, source_target_pairs={{0,2},{2,4},{4,6},{6,0},{1,3},{3,5},{5,7},{7,1},{8,10},{10,12},{12... | collective-permute-start | bytes 983048 | tf_op jit(solution)/shard_map/ppermute | solution.py:407
  17.1 10.7 %collective-permute-start.5 = (f32[2,32,1280]{2,1,0:T(8,128)}, f32[2,32,1280]{2,1,0:T(8,128)}, u32[]{:S(2)}, u32[]{:S(2)}) collective-permute-start(f32[2,32,1280]{2,1,0:T(8,128)} %bitcast_add_fusion.1), channel_id=1, source_target_pairs={{0,6},{2,0},{4,2},{6,4},{1,7},{3,1},{5,3},{7,5},{8,14},{10,8},{12,... | collective-permute-start | bytes 983048 | tf_op jit(solution)/shard_map/ppermute | solution.py:407
  21.0 23.4 %copy-start.7 = (s32[4096,32]{0,1:T(8,128)S(1)}, s32[4096,32]{0,1:T(8,128)}, u32[]{:S(2)}) copy-start(s32[4096,32]{0,1:T(8,128)} %param.12) | copy-start | bytes 1572868
  21.0 18.4 %collective-permute-start.7 = (f32[4,32,1536]{2,1,0:T(8,128)S(1)}, f32[4,32,1536]{2,1,0:T(8,128)S(1)}, u32[]{:S(2)}, u32[]{:S(2)}) collective-permute-start(f32[4,32,1536]{2,1,0:T(8,128)S(1)} %fusion), channel_id=1, source_target_pairs={{0,1},{1,0},{2,3},{3,2},{4,5},{5,4},{6,7},{7,6},{8,9},{9,8},{10,11... | collective-permute-start | bytes 2359304 | tf_op jit(solution)/shard_map/ppermute | solution.py:411
  27.8 21.9 %copy-start = (bf16[256,512]{1,0:T(8,128)(2,1)S(1)}, bf16[256,512]{1,0:T(8,128)(2,1)}, u32[]{:S(2)}) copy-start(bf16[256,512]{1,0:T(8,128)(2,1)} %constant.73.clone.refs_7_.forth_ref) | copy-start | bytes 786436
  27.8 21.9 %copy-start.5 = (f32[2,32,128]{2,1,0:T(8,128)S(1)}, f32[2,32,128]{2,1,0:T(8,128)}, u32[]{:S(2)}) copy-start(f32[2,32,128]{2,1,0:T(8,128)} %constant.72.clone.refs_6_.turn_ref) | copy-start | bytes 98308
  29.4 17.6 %collective-permute-start.6 = (f32[32,2560]{1,0:T(8,128)S(1)}, f32[32,2560]{1,0:T(8,128)S(1)}, u32[]{:S(2)}, u32[]{:S(2)}) collective-permute-start(f32[32,2560]{1,0:T(8,128)S(1)} %get-tuple-element.29), channel_id=1, source_target_pairs={{0,1},{1,0},{2,3},{3,2},{4,5},{5,4},{6,7},{7,6},{8,9},{9,8},{10,11... | collective-permute-start | bytes 983048 | tf_op jit(solution)/shard_map/ppermute | solution.py:411
  41.4 6.6 %collective-permute-start.10 = (f32[32,1536]{1,0:T(8,128)}, f32[32,1536]{1,0:T(8,128)S(1)}, u32[]{:S(2)}, u32[]{:S(2)}) collective-permute-start(f32[32,1536]{1,0:T(8,128)} %get-tuple-element.25), channel_id=1, source_target_pairs={{0,4},{2,6},{4,0},{6,2},{1,5},{3,7},{5,1},{7,3},{8,12},{10,14},{12... | collective-permute-start | bytes 589832 | tf_op jit(solution)/shard_map/ppermute | solution.py:407
  41.7 8.0 %collective-permute-start.8 = (f32[32,1536]{1,0:T(8,128)}, f32[32,1536]{1,0:T(8,128)S(1)}, u32[]{:S(2)}, u32[]{:S(2)}) collective-permute-start(f32[32,1536]{1,0:T(8,128)} %get-tuple-element.27), channel_id=1, source_target_pairs={{0,2},{2,4},{4,6},{6,0},{1,3},{3,5},{5,7},{7,1},{8,10},{10,12},{12... | collective-permute-start | bytes 589832 | tf_op jit(solution)/shard_map/ppermute | solution.py:407
  42.1 7.7 %collective-permute-start.9 = (f32[32,1536]{1,0:T(8,128)S(1)}, f32[32,1536]{1,0:T(8,128)S(1)}, u32[]{:S(2)}, u32[]{:S(2)}) collective-permute-start(f32[32,1536]{1,0:T(8,128)S(1)} %get-tuple-element.26), channel_id=1, source_target_pairs={{0,6},{2,0},{4,2},{6,4},{1,7},{3,1},{5,3},{7,5},{8,14},{10,8},{12,... | collective-permute-start | bytes 589832 | tf_op jit(solution)/shard_map/ppermute | solution.py:407
  51.2 35.8 %copy-start.1 = (bf16[256,512]{1,0:T(8,128)(2,1)S(1)}, bf16[256,512]{1,0:T(8,128)(2,1)}, u32[]{:S(2)}) copy-start(bf16[256,512]{1,0:T(8,128)(2,1)} %constant.75.clone.back_ref) | copy-start | bytes 786436
  51.2 35.8 %copy-start.2 = (bf16[512,256]{1,0:T(8,128)(2,1)S(1)}, bf16[512,256]{1,0:T(8,128)(2,1)}, u32[]{:S(2)}) copy-start(bf16[512,256]{1,0:T(8,128)(2,1)} %constant.76.clone.short_forth_ref) | copy-start | bytes 786436
  51.2 35.8 %copy-start.3 = (bf16[512,256]{1,0:T(8,128)(2,1)S(1)}, bf16[512,256]{1,0:T(8,128)(2,1)}, u32[]{:S(2)}) copy-start(bf16[512,256]{1,0:T(8,128)(2,1)} %constant.77.clone.short_back_ref) | copy-start | bytes 786436
  51.2 35.8 %copy-start.6 = (f32[2,128,128]{2,1,0:T(8,128)S(1)}, f32[2,128,128]{2,1,0:T(8,128)}, u32[]{:S(2)}) copy-start(f32[2,128,128]{2,1,0:T(8,128)} %constant.74.clone.turn_ref) | copy-start | bytes 393220
  51.2 35.8 %all-to-all-start = ((f32[128,1,1152]{2,1,0:T(1,128)}), f32[128,1,1152]{2,1,0:T(1,128)S(1)}, u32[]{:S(2)}, u32[]{:S(2)}) async-start(f32[128,1,1152]{2,1,0:T(1,128)} %bitcast.19), calls=%async_computation | async-start | bytes 1179648 | tf_op jit(solution)/shard_map/all_to_all | solution.py:402
  68.4 18.6 %collective-permute-start.11 = (s32[512,128]{1,0:T(8,128)S(1)}, s32[512,128]{1,0:T(8,128)S(1)}, u32[]{:S(2)}, u32[]{:S(2)}) collective-permute-start(s32[512,128]{1,0:T(8,128)S(1)} %copy.29), channel_id=1, source_target_pairs={{0,127},{1,126},{2,125},{3,124},{4,123},{5,122},{6,121},{7,120},{8... | collective-permute-start | bytes 786440 | tf_op jit(solution)/shard_map/ppermute | solution.py:468
  76.6 41.2 %copy-start.4 = (bf16[512,256]{1,0:T(8,128)(2,1)S(1)}, bf16[512,256]{1,0:T(8,128)(2,1)}, u32[]{:S(2)}) copy-start(bf16[512,256]{1,0:T(8,128)(2,1)} %constant.78.clone.table_ref) | copy-start | bytes 786436

commit v3 on v2

--- a/solution.py
+++ b/solution.py
@@ -219,7 +219,6 @@
     short_forth_ref,
     short_back_ref,
     out_ref,
-    power_ref,
     bands_ref,
 ):
     lane = lax.broadcasted_iota(jnp.int32, (LONG, LONG), 1)
@@ -272,6 +271,30 @@
                 jnp.concatenate([real * cosine - imag * sine, imag * cosine + real * sine], axis=0)
             )
         return table_times(back_ref, jnp.concatenate(columns, axis=1))
+
+    bands_ref[...] = jnp.zeros_like(bands_ref)
+
+    def counted(group, power, mirror_power):
+        rows = slice(LONG * group, LONG * group + LONG)
+        mirror_bins = mirror_ref[rows]
+        if group == 0:
+            mirror_bins = jnp.where(lone, middle_ref[...], mirror_bins)
+        for got, bins in ((power, bins_ref[rows]), (mirror_power, mirror_bins)):
+            high = got.astype(BF16).astype(jnp.float32)
+            low = got - high
+            coarse, fine = bins >> 3, bins & 7
+            values, marks = [], []
+            for start in range(0, LONG, 8):
+                here = slice(start, start + 8)
+                chosen = [coarse[here] == index for index in range(8)]
+                stack = [jnp.where(mask, high[here], 0.0) for mask in chosen]
+                stack += [jnp.where(mask, low[here], 0.0) for mask in chosen]
+                values.append(jnp.concatenate(stack, axis=0).astype(BF16))
+                stack = [jnp.where(fine[here] == index, 1.0, 0.0) for index in range(8)]
+                marks.append(jnp.concatenate(stack, axis=0).astype(BF16))
+            bands_ref[...] += product(
+                jnp.concatenate(values, axis=1), jnp.concatenate(marks, axis=1), ((1,), (1,))
+            )
 
     middle = arrived_ref[pl.ds(8, LONG, FORTH), :]
     tile = (jnp.where(lone, middle, 0.0), jnp.where(lone, pltpu.roll(middle, 96, 1), 0.0))
@@ -297,8 +320,7 @@
                 b_real = jnp.where(lone, middle_hat[0], b_real)
                 b_imag = jnp.where(lone, middle_hat[1], b_imag)
                 mirror_power = jnp.where(lone, middle_power, power)
-            power_ref[LONG * group : LONG * group + LONG, :] = power
-            power_ref[LONG * (4 + group) : LONG * (5 + group), :] = mirror_power
+            counted(group, power, mirror_power)
             hats_a.append(
                 jnp.concatenate(
                     [kernel_real * real - odd * imag, kernel_real * imag + odd * real], axis=1
@@ -314,30 +336,24 @@
                         LONG * part : LONG * part + LONG, LONG * side : LONG * side + LONG
                     ]
 
-    def counted(tile_ref, offset, inner=None):
-        def one_block(block, carry):
-            start = pl.multiple_of(block * 64, 64)
-            power = power_ref[pl.ds(offset + start, 64), :]
-            bins = tile_ref[pl.ds(start, 64), :]
-            if inner is not None:
-                row = jnp.minimum(start, LONG - 64)
-                here = (lane[:64] < SHORT) & (start < LONG)
-                bins = jnp.where(here, inner[pl.ds(pl.multiple_of(row, 64), 64), :], bins)
-            for band in range(NBINS):
-                chosen = jnp.where(bins == band, power, 0.0)
-                bands_ref[8 * band : 8 * band + 8, :] += jnp.sum(
-                    chosen.reshape(8, 8, LONG), axis=0
-                )
-            return carry
-
-        lax.fori_loop(0, 4 * LONG // 64, one_block, 0)
-
-    bands_ref[...] = jnp.zeros_like(bands_ref)
-    counted(bins_ref, 0)
-    counted(mirror_ref, 4 * LONG, middle_ref)
-    sums = jnp.sum(bands_ref[...].reshape(NBINS, 8, LONG), axis=1)
-    sums = jnp.concatenate([sums, jnp.zeros((LONG - NBINS, LONG), jnp.float32)], axis=0)
-    line = jnp.sum(sums.T, axis=0, keepdims=True) * (NBINS / float(N) ** 4)
+    row = lax.broadcasted_iota(jnp.int32, (LONG, NBINS), 0)
+    column = lax.broadcasted_iota(jnp.int32, (LONG, NBINS), 1)
+    sums = jnp.where(row % 8 == column % 8, bands_ref[...], 0.0)
+    sums = jnp.sum(sums.reshape(2, 8, 8, NBINS).sum(axis=0), axis=1)
+    left = lax.broadcasted_iota(jnp.int32, (NBINS, LONG), 0)
+    right = lax.broadcasted_iota(jnp.int32, (NBINS, LONG), 1)
+    gather = jnp.where((left // 8 == right % 8) & (right < NBINS), 1.0, 0.0)
+    sums = lax.dot_general(
+        sums,
+        gather,
+        (((1,), (0,)), ((), ())),
+        precision=lax.Precision.HIGHEST,
+        preferred_element_type=jnp.float32,
+    )
+    coarse = lax.broadcasted_iota(jnp.int32, (8, LONG), 0)
+    lanes = lax.broadcasted_iota(jnp.int32, (8, LONG), 1)
+    line = jnp.sum(jnp.where(lanes // 8 == coarse, sums, 0.0), axis=0, keepdims=True)
+    line = line * (NBINS / float(N) ** 4)
     out_ref[pl.ds(16, LONG, BACK), :] = jnp.broadcast_to(line, (LONG, LONG))
 
 
@@ -489,7 +505,7 @@
     sent = call(
         columns_kernel,
         f32(LONG * BACK, LONG),
-        [pltpu.VMEM((8 * LONG, LONG), jnp.float32), pltpu.VMEM((8 * NBINS, LONG), jnp.float32)],
+        [pltpu.VMEM((LONG, NBINS), jnp.float32)],
         (
             (device * SHORT).reshape(1),
             arrived,

time: 120 us -> 118 us (0.983)
  Pallas kernels: 9.69 us -> 7.36 us
    pallas_call x3, Pallas kernels: 9.69 us -> 7.36 us  [call(): pl.pallas_call(kernel, out_shape=outs, in_specs=specs, out_specs=jax.tree...]
where the time goes in v3:
time: 118 us; the launch traced here: 117 us
  starting transfers between devices  41.8 us (35%)
  waiting for transfers between devices  28.2 us (24%)
  blocking collectives  24.4 us (21%)
  other arithmetic  9 us (8%)
  Pallas kernels  7.36 us (6%)
  local copies, waits for them, and re-layouts  5.08 us (4%)
  between operations  1.55 us (1%)
    all_to_all x1, blocking collectives, exchanged(): lax.all_to_all(blocks, ROWS_PLANES, split_axis=0, concat_axis=0, tiled=True)  24.4 us
    all_to_all x1, starting transfers between devices, exchanged(): lax.all_to_all(blocks, ROWS_PLANES, split_axis=0, concat_axis=0, tiled=True)  15.8 us
    ppermute x9, waiting for transfers between devices, along(): lax.ppermute(array, PLANES[0], [(i, (i + step) % 4) for i in range(4)])  11.7 us
    ppermute x9, starting transfers between devices, along(): lax.ppermute(array, PLANES[0], [(i, (i + step) % 4) for i in range(4)])  10.8 us
    ppermute x1, waiting for transfers between devices, swapped_mirror(): lax.ppermute(array, ROWS_PLANES, [(i, LONG - 1 - i) for i in range(LONG)])  10 us
    ppermute x1, starting transfers between devices, swapped_mirror(): lax.ppermute(array, ROWS_PLANES, [(i, LONG - 1 - i) for i in range(LONG)])  8.05 us
    pallas_call x3, Pallas kernels, call(): pl.pallas_call(kernel, out_shape=outs, in_specs=specs, out_specs=jax.tree...  7.36 us
    ppermute x2, starting transfers between devices, swapped(): return lax.ppermute(array, PLANES[1], [(0, 1), (1, 0)])  7.12 us
  transfers between devices with their start and end apart: 13, of which 6 were waited for; matrix products, arithmetic and copies ran while one was open for 11% of the time, Pallas kernels for 0%

profile of v3, /device:TPU:1, one launch (start us, length us, event | category | flops | bytes accessed | tf_op | source)
XLA Modules:
  0.0 117.3 jit_solution(17688623744784351334)
XLA Ops:
  1.3 1.4 %multiply_bitcast_fusion.1 = (f32[2,32,1280]{2,1,0:T(8,128)S(1)}, f32[2,32,1280]{2,1,0:T(8,128)S(1)}, f32[2,32,1280]{2,1,0:T(8,128)S(1)}, f32[2,32,1280]{2,1,0:T(8,128)S(1)}) fusion(f32[4,2,32,4096]{3,2,1,0:T(8,128)} %bitcast.85, s32[]{:T(128)S(6)} %select_n.31, f32[]{:T(128)} %bitcast.81, s32[]{:T(128)S(6)} %select_n.30, s32[]{:T(128)S(6)} %select_n.33), kind=kLoop, calls=%fused_computation.18 | loop fusion | flops 327680 | bytes 2621456 | tf_op jit(solution)/shard_map/mul | solution.py:445
  2.7 2.2 %collective-permute-start = (f32[2,32,1280]{2,1,0:T(8,128)S(1)}, f32[2,32,1280]{2,1,0:T(8,128)S(1)}, u32[]{:S(2)}, u32[]{:S(2)}) collective-permute-start(f32[2,32,1280]{2,1,0:T(8,128)S(1)} %get-tuple-element.24), channel_id=1, source_target_pairs={{0,2},{2,4},{4,6},{6,0},{1,3},{3,5},{5,7},{7,1},{8,10},{10,12},{12... | collective-permute-start | bytes 983048 | tf_op jit(solution)/shard_map/ppermute | solution.py:423
  4.9 1.5 %collective-permute-start.4 = (f32[2,32,1280]{2,1,0:T(8,128)S(1)}, f32[2,32,1280]{2,1,0:T(8,128)S(1)}, u32[]{:S(2)}, u32[]{:S(2)}) collective-permute-start(f32[2,32,1280]{2,1,0:T(8,128)S(1)} %get-tuple-element.22), channel_id=1, source_target_pairs={{0,6},{2,0},{4,2},{6,4},{1,7},{3,1},{5,3},{7,5},{8,14},{10,8},{12,... | collective-permute-start | bytes 983048 | tf_op jit(solution)/shard_map/ppermute | solution.py:423
  6.4 1.4 %collective-permute-start.2 = (f32[2,32,1280]{2,1,0:T(8,128)S(1)}, f32[2,32,1280]{2,1,0:T(8,128)S(1)}, u32[]{:S(2)}, u32[]{:S(2)}) collective-permute-start(f32[2,32,1280]{2,1,0:T(8,128)S(1)} %get-tuple-element.23), channel_id=1, source_target_pairs={{0,6},{2,0},{4,2},{6,4},{1,7},{3,1},{5,3},{7,5},{8,14},{10,8},{12,... | collective-permute-start | bytes 983048 | tf_op jit(solution)/shard_map/ppermute | solution.py:423
  7.8 5.8 %collective-permute-done = f32[2,32,1280]{2,1,0:T(8,128)S(1)} collective-permute-done((f32[2,32,1280]{2,1,0:T(8,128)S(1)}, f32[2,32,1280]{2,1,0:T(8,128)S(1)}, u32[]{:S(2)}, u32[]{:S(2)}) %collective-permute-start) | collective-permute-done | bytes 327712 | tf_op jit(solution)/shard_map/ppermute | solution.py:423
  13.6 1.7 %bitcast_add_fusion.4 = f32[2,32,1280]{2,1,0:T(8,128)} fusion(f32[2,32,1280]{2,1,0:T(8,128)S(1)} %collective-permute-done, f32[4,2,32,4096]{3,2,1,0:T(8,128)} %bitcast.86, s32[]{:T(128)S(6)} %select_n.31, f32[]{:T(128)} %bitcast.80), kind=kLoop, calls=%fused_computation.16 | loop fusion | flops 163840 | bytes 983048 | tf_op jit(solution)/shard_map/add | solution.py:457
  15.4 1.7 %bitcast_add_fusion.1 = f32[2,32,1280]{2,1,0:T(8,128)} fusion(f32[2,32,1280]{2,1,0:T(8,128)S(1)} %collective-permute-done.4, f32[4,2,32,4096]{3,2,1,0:T(8,128)} %bitcast.87, s32[]{:T(128)S(6)} %select_n.33, f32[]{:T(128)} %bitcast.79), kind=kLoop, calls=%fused_computation.11 | loop fusion | flops 163840 | bytes 983048 | tf_op jit(solution)/shard_map/add | solution.py:458
  17.1 2.7 %collective-permute-start.5 = (f32[2,32,1280]{2,1,0:T(8,128)}, f32[2,32,1280]{2,1,0:T(8,128)}, u32[]{:S(2)}, u32[]{:S(2)}) collective-permute-start(f32[2,32,1280]{2,1,0:T(8,128)} %bitcast_add_fusion.1), channel_id=1, source_target_pairs={{0,6},{2,0},{4,2},{6,4},{1,7},{3,1},{5,3},{7,5},{8,14},{10,8},{12,... | collective-permute-start | bytes 983048 | tf_op jit(solution)/shard_map/ppermute | solution.py:423
  19.8 1.2 %fusion = f32[4,32,1536]{2,1,0:T(8,128)S(1)} fusion(f32[4,2,32,4096]{3,2,1,0:T(8,128)} %bitcast.88, s32[]{:T(128)S(6)} %select_n.35, f32[]{:T(128)} %bitcast.77), kind=kLoop, calls=%fused_computation.1 | loop fusion | flops 196608 | bytes 1572872 | tf_op jit(solution)/shard_map/mul | solution.py:449
  21.0 3.6 %collective-permute-start.7 = (f32[4,32,1536]{2,1,0:T(8,128)S(1)}, f32[4,32,1536]{2,1,0:T(8,128)S(1)}, u32[]{:S(2)}, u32[]{:S(2)}) collective-permute-start(f32[4,32,1536]{2,1,0:T(8,128)S(1)} %fusion), channel_id=1, source_target_pairs={{0,1},{1,0},{2,3},{3,2},{4,5},{5,4},{6,7},{7,6},{8,9},{9,8},{10,11... | collective-permute-start | bytes 2359304 | tf_op jit(solution)/shard_map/ppermute | solution.py:427
  24.5 3.2 %collective-permute-done.1 = f32[2,32,1280]{2,1,0:T(8,128)} collective-permute-done((f32[2,32,1280]{2,1,0:T(8,128)}, f32[2,32,1280]{2,1,0:T(8,128)}, u32[]{:S(2)}, u32[]{:S(2)}) %collective-permute-start.1) | collective-permute-done | bytes 327712 | tf_op jit(solution)/shard_map/ppermute | solution.py:423
  27.8 1.5 %fusion.5 = (f32[2,32,1280]{2,1,0:T(8,128)S(1)}, f32[2,32,1280]{2,1,0:T(8,128)S(1)}) fusion(f32[2,32,1280]{2,1,0:T(8,128)} %collective-permute-done.5, f32[2,32,1280]{2,1,0:T(8,128)} %collective-permute-done.3, f32[4,2,32,4096]{3,2,1,0:T(8,128)} %bitcast.89, s32[]{:T(128)S(6)} %select_n.32, f32[]{:T(128)} %bitcast.76, ...), kind=kLoop, calls=%fused_computation.13 | loop fusion | flops 491520 | bytes 2621448 | tf_op jit(solution)/shard_map/add | solution.py:469
  29.4 3.6 %collective-permute-start.6 = (f32[32,2560]{1,0:T(8,128)S(1)}, f32[32,2560]{1,0:T(8,128)S(1)}, u32[]{:S(2)}, u32[]{:S(2)}) collective-permute-start(f32[32,2560]{1,0:T(8,128)S(1)} %get-tuple-element.29), channel_id=1, source_target_pairs={{0,1},{1,0},{2,3},{3,2},{4,5},{5,4},{6,7},{7,6},{8,9},{9,8},{10,11... | collective-permute-start | bytes 983048 | tf_op jit(solution)/shard_map/ppermute | solution.py:427
  32.9 6.4 %collective-permute-done.7 = f32[4,32,1536]{2,1,0:T(8,128)S(1)} collective-permute-done((f32[4,32,1536]{2,1,0:T(8,128)S(1)}, f32[4,32,1536]{2,1,0:T(8,128)S(1)}, u32[]{:S(2)}, u32[]{:S(2)}) %collective-permute-start.7) | collective-permute-done | bytes 786464 | tf_op jit(solution)/shard_map/ppermute | solution.py:427
  39.4 1.2 %bitcast_add_fusion = f32[4,32,1536]{2,1,0:T(8,128)S(1)} fusion(f32[4,32,1536]{2,1,0:T(8,128)S(1)} %collective-permute-done.7, s32[]{:T(128)S(6)} %select_n.34, f32[]{:T(128)} %bitcast.78, f32[4,2,32,4096]{3,2,1,0:T(8,128)} %bitcast.90), kind=kLoop, calls=%fused_computation.2 | loop fusion | flops 393216 | bytes 2359812 | tf_op jit(solution)/shard_map/add | solution.py:459
  40.6 0.8 dynamic-slice_bitcast_fusion
  41.4 0.2 collective-permute-start.10
  41.7 0.4 collective-permute-start.8
  42.1 2.3 %collective-permute-start.9 = (f32[32,1536]{1,0:T(8,128)S(1)}, f32[32,1536]{1,0:T(8,128)S(1)}, u32[]{:S(2)}, u32[]{:S(2)}) collective-permute-start(f32[32,1536]{1,0:T(8,128)S(1)} %get-tuple-element.26), channel_id=1, source_target_pairs={{0,6},{2,0},{4,2},{6,4},{1,7},{3,1},{5,3},{7,5},{8,14},{10,8},{12,... | collective-permute-start | bytes 589832 | tf_op jit(solution)/shard_map/ppermute | solution.py:423
  44.5 2.3 %reverse.2 = s32[15,4096]{1,0:T(8,128)S(1)} reverse(s32[15,4096]{1,0:T(8,128)S(1)} %bitcast.91), dimensions={1} | reverse | bytes 491520
  46.8 0.2 slice.36
  47.0 1.0 collective-permute-done.10.refs_5_
  48.0 1.7 %collective-permute-done.8.refs_3_ = f32[32,1536]{1,0:T(8,128)S(1)} collective-permute-done((f32[32,1536]{1,0:T(8,128)}, f32[32,1536]{1,0:T(8,128)S(1)}, u32[]{:S(2)}, u32[]{:S(2)}) %collective-permute-start.8) | collective-permute-done | bytes 196640 | tf_op jit(solution)/shard_map/ppermute | solution.py:423
  49.7 1.5 %shard_map.121 = f32[1152,128]{1,0:T(8,128)} custom-call(f32[32,2560]{1,0:T(8,128)S(1)} %get-tuple-element.30.refs_0_, f32[32,2560]{1,0:T(8,128)S(1)} %collective-permute-done.6.refs_1_, f32[32,1536]{1,0:T(8,128)S(1)} %get-tuple-element.28.refs_2_, f32[32,1536]{1,0:T(8,128)S(1)} %collective-permute-done.8.refs_3_, ...), custom_call_target="tpu_custom_call" | custom-call | tf_op jit(solution)/shard_map/pallas_call | solution.py:402
  51.2 15.8 %all-to-all-start = ((f32[128,1,1152]{2,1,0:T(1,128)}), f32[128,1,1152]{2,1,0:T(1,128)S(1)}, u32[]{:S(2)}, u32[]{:S(2)}) async-start(f32[128,1,1152]{2,1,0:T(1,128)} %bitcast.19), calls=%async_computation | async-start | bytes 1179648 | tf_op jit(solution)/shard_map/all_to_all | solution.py:418
  67.2 0.8 rev.4
  68.1 0.2 copy.28
  68.4 8.1 %collective-permute-start.11 = (s32[512,128]{1,0:T(8,128)S(1)}, s32[512,128]{1,0:T(8,128)S(1)}, u32[]{:S(2)}, u32[]{:S(2)}) collective-permute-start(s32[512,128]{1,0:T(8,128)S(1)} %copy.29), channel_id=1, source_target_pairs={{0,127},{1,126},{2,125},{3,124},{4,123},{5,122},{6,121},{7,120},{8... | collective-permute-start | bytes 786440 | tf_op jit(solution)/shard_map/ppermute | solution.py:484
  77.0 10.0 %collective-permute-done.11.mirror_ref = s32[512,128]{1,0:T(8,128)S(1)} collective-permute-done((s32[512,128]{1,0:T(8,128)S(1)}, s32[512,128]{1,0:T(8,128)S(1)}, u32[]{:S(2)}, u32[]{:S(2)}) %collective-permute-start.11) | collective-permute-done | bytes 262176 | tf_op jit(solution)/shard_map/ppermute | solution.py:484
  87.0 4.0 %shard_map.122 = f32[2176,128]{1,0:T(8,128)S(1)} custom-call(s32[1]{0:T(128)} %bitcast.first_ref, f32[1152,128]{1,0:T(8,128)S(1)} %bitcast.84, s32[512,128]{1,0:T(8,128)S(1)} %copy.31.bins_ref, s32[512,128]{1,0:T(8,128)S(1)} %collective-permute-done.11.mirror_ref, s32[128,128]{1,0:T(8,128)S(1)} %pad.4.middle_ref, f32[2,128,128]{2,1,0:T(8,128)S(1)} %copy-done.6, ...), custom_call_target="tpu_custom_call" | custom-call | tf_op jit(solution)/shard_map/pallas_call | solution.py:402
  91.0 24.4 %all_to_all.10 = f32[128,1,2176]{2,1,0:T(1,128)S(1)} all-to-all(f32[128,1,2176]{2,1,0:T(1,128)S(1)} %bitcast.83), channel_id=1, replica_groups=mesh['rows_0'=4,'rows_1'=2,'rows_2'=2,'planes_0'=4,'planes_1'=2] {'rows_..., dimensions={0} | all-to-all | bytes 2228224 | tf_op jit(solution)/shard_map/all_to_all | solution.py:418
  115.4 1.9 %shard_map.123 = (f32[32,4096]{1,0:T(8,128)}, f32[32,4096]{1,0:T(8,128)}, f32[1,64]{1,0:T(1,128)}) custom-call(f32[2176,128]{1,0:T(8,128)S(1)} %bitcast.82, f32[2,32,128]{2,1,0:T(8,128)S(1)} %copy-done.5, bf16[512,256]{1,0:T(8,128)(2,1)S(1)} %copy-done.4), custom_call_target="tpu_custom_call" | custom-call | tf_op jit(solution)/shard_map/pallas_call | solution.py:402
  (41 shorter events, 1.2 us)
Async XLA Ops:
  2.7 10.9 %collective-permute-start = (f32[2,32,1280]{2,1,0:T(8,128)S(1)}, f32[2,32,1280]{2,1,0:T(8,128)S(1)}, u32[]{:S(2)}, u32[]{:S(2)}) collective-permute-start(f32[2,32,1280]{2,1,0:T(8,128)S(1)} %get-tuple-element.24), channel_id=1, source_target_pairs={{0,2},{2,4},{4,6},{6,0},{1,3},{3,5},{5,7},{7,1},{8,10},{10,12},{12... | collective-permute-start | bytes 983048 | tf_op jit(solution)/shard_map/ppermute | solution.py:423
  4.9 10.5 %collective-permute-start.4 = (f32[2,32,1280]{2,1,0:T(8,128)S(1)}, f32[2,32,1280]{2,1,0:T(8,128)S(1)}, u32[]{:S(2)}, u32[]{:S(2)}) collective-permute-start(f32[2,32,1280]{2,1,0:T(8,128)S(1)} %get-tuple-element.22), channel_id=1, source_target_pairs={{0,6},{2,0},{4,2},{6,4},{1,7},{3,1},{5,3},{7,5},{8,14},{10,8},{12,... | collective-permute-start | bytes 983048 | tf_op jit(solution)/shard_map/ppermute | solution.py:423
  6.4 21.4 %collective-permute-start.2 = (f32[2,32,1280]{2,1,0:T(8,128)S(1)}, f32[2,32,1280]{2,1,0:T(8,128)S(1)}, u32[]{:S(2)}, u32[]{:S(2)}) collective-permute-start(f32[2,32,1280]{2,1,0:T(8,128)S(1)} %get-tuple-element.23), channel_id=1, source_target_pairs={{0,6},{2,0},{4,2},{6,4},{1,7},{3,1},{5,3},{7,5},{8,14},{10,8},{12,... | collective-permute-start | bytes 983048 | tf_op jit(solution)/shard_map/ppermute | solution.py:423
  7.8 20.0 %collective-permute-start.3 = (f32[2,32,1280]{2,1,0:T(8,128)S(1)}, f32[2,32,1280]{2,1,0:T(8,128)}, u32[]{:S(2)}, u32[]{:S(2)}) collective-permute-start(f32[2,32,1280]{2,1,0:T(8,128)S(1)} %get-tuple-element.21), channel_id=1, source_target_pairs={{0,2},{2,4},{4,6},{6,0},{1,3},{3,5},{5,7},{7,1},{8,10},{10,12},{12... | collective-permute-start | bytes 983048 | tf_op jit(solution)/shard_map/ppermute | solution.py:423
  15.3 12.4 %collective-permute-start.1 = (f32[2,32,1280]{2,1,0:T(8,128)}, f32[2,32,1280]{2,1,0:T(8,128)}, u32[]{:S(2)}, u32[]{:S(2)}) collective-permute-start(f32[2,32,1280]{2,1,0:T(8,128)} %bitcast_add_fusion.4), channel_id=1, source_target_pairs={{0,2},{2,4},{4,6},{6,0},{1,3},{3,5},{5,7},{7,1},{8,10},{10,12},{12... | collective-permute-start | bytes 983048 | tf_op jit(solution)/shard_map/ppermute | solution.py:423
  17.1 10.7 %collective-permute-start.5 = (f32[2,32,1280]{2,1,0:T(8,128)}, f32[2,32,1280]{2,1,0:T(8,128)}, u32[]{:S(2)}, u32[]{:S(2)}) collective-permute-start(f32[2,32,1280]{2,1,0:T(8,128)} %bitcast_add_fusion.1), channel_id=1, source_target_pairs={{0,6},{2,0},{4,2},{6,4},{1,7},{3,1},{5,3},{7,5},{8,14},{10,8},{12,... | collective-permute-start | bytes 983048 | tf_op jit(solution)/shard_map/ppermute | solution.py:423
  21.0 23.4 %copy-start.7 = (s32[4096,32]{0,1:T(8,128)S(1)}, s32[4096,32]{0,1:T(8,128)}, u32[]{:S(2)}) copy-start(s32[4096,32]{0,1:T(8,128)} %param.12) | copy-start | bytes 1572868
  21.0 18.4 %collective-permute-start.7 = (f32[4,32,1536]{2,1,0:T(8,128)S(1)}, f32[4,32,1536]{2,1,0:T(8,128)S(1)}, u32[]{:S(2)}, u32[]{:S(2)}) collective-permute-start(f32[4,32,1536]{2,1,0:T(8,128)S(1)} %fusion), channel_id=1, source_target_pairs={{0,1},{1,0},{2,3},{3,2},{4,5},{5,4},{6,7},{7,6},{8,9},{9,8},{10,11... | collective-permute-start | bytes 2359304 | tf_op jit(solution)/shard_map/ppermute | solution.py:427
  27.8 21.9 %copy-start = (bf16[256,512]{1,0:T(8,128)(2,1)S(1)}, bf16[256,512]{1,0:T(8,128)(2,1)}, u32[]{:S(2)}) copy-start(bf16[256,512]{1,0:T(8,128)(2,1)} %constant.73.clone.refs_7_.forth_ref) | copy-start | bytes 786436
  27.8 21.9 %copy-start.5 = (f32[2,32,128]{2,1,0:T(8,128)S(1)}, f32[2,32,128]{2,1,0:T(8,128)}, u32[]{:S(2)}) copy-start(f32[2,32,128]{2,1,0:T(8,128)} %constant.72.clone.refs_6_.turn_ref) | copy-start | bytes 98308
  29.4 17.6 %collective-permute-start.6 = (f32[32,2560]{1,0:T(8,128)S(1)}, f32[32,2560]{1,0:T(8,128)S(1)}, u32[]{:S(2)}, u32[]{:S(2)}) collective-permute-start(f32[32,2560]{1,0:T(8,128)S(1)} %get-tuple-element.29), channel_id=1, source_target_pairs={{0,1},{1,0},{2,3},{3,2},{4,5},{5,4},{6,7},{7,6},{8,9},{9,8},{10,11... | collective-permute-start | bytes 983048 | tf_op jit(solution)/shard_map/ppermute | solution.py:427
  41.4 6.6 %collective-permute-start.10 = (f32[32,1536]{1,0:T(8,128)}, f32[32,1536]{1,0:T(8,128)S(1)}, u32[]{:S(2)}, u32[]{:S(2)}) collective-permute-start(f32[32,1536]{1,0:T(8,128)} %get-tuple-element.25), channel_id=1, source_target_pairs={{0,4},{2,6},{4,0},{6,2},{1,5},{3,7},{5,1},{7,3},{8,12},{10,14},{12... | collective-permute-start | bytes 589832 | tf_op jit(solution)/shard_map/ppermute | solution.py:423
  41.7 8.0 %collective-permute-start.8 = (f32[32,1536]{1,0:T(8,128)}, f32[32,1536]{1,0:T(8,128)S(1)}, u32[]{:S(2)}, u32[]{:S(2)}) collective-permute-start(f32[32,1536]{1,0:T(8,128)} %get-tuple-element.27), channel_id=1, source_target_pairs={{0,2},{2,4},{4,6},{6,0},{1,3},{3,5},{5,7},{7,1},{8,10},{10,12},{12... | collective-permute-start | bytes 589832 | tf_op jit(solution)/shard_map/ppermute | solution.py:423
  42.1 7.7 %collective-permute-start.9 = (f32[32,1536]{1,0:T(8,128)S(1)}, f32[32,1536]{1,0:T(8,128)S(1)}, u32[]{:S(2)}, u32[]{:S(2)}) collective-permute-start(f32[32,1536]{1,0:T(8,128)S(1)} %get-tuple-element.26), channel_id=1, source_target_pairs={{0,6},{2,0},{4,2},{6,4},{1,7},{3,1},{5,3},{7,5},{8,14},{10,8},{12,... | collective-permute-start | bytes 589832 | tf_op jit(solution)/shard_map/ppermute | solution.py:423
  51.2 35.8 %copy-start.1 = (bf16[256,512]{1,0:T(8,128)(2,1)S(1)}, bf16[256,512]{1,0:T(8,128)(2,1)}, u32[]{:S(2)}) copy-start(bf16[256,512]{1,0:T(8,128)(2,1)} %constant.75.clone.back_ref) | copy-start | bytes 786436
  51.2 35.8 %copy-start.2 = (bf16[512,256]{1,0:T(8,128)(2,1)S(1)}, bf16[512,256]{1,0:T(8,128)(2,1)}, u32[]{:S(2)}) copy-start(bf16[512,256]{1,0:T(8,128)(2,1)} %constant.76.clone.short_forth_ref) | copy-start | bytes 786436
  51.2 35.8 %copy-start.3 = (bf16[512,256]{1,0:T(8,128)(2,1)S(1)}, bf16[512,256]{1,0:T(8,128)(2,1)}, u32[]{:S(2)}) copy-start(bf16[512,256]{1,0:T(8,128)(2,1)} %constant.77.clone.short_back_ref) | copy-start | bytes 786436
  51.2 35.8 %copy-start.6 = (f32[2,128,128]{2,1,0:T(8,128)S(1)}, f32[2,128,128]{2,1,0:T(8,128)}, u32[]{:S(2)}) copy-start(f32[2,128,128]{2,1,0:T(8,128)} %constant.74.clone.turn_ref) | copy-start | bytes 393220
  51.2 35.8 %all-to-all-start = ((f32[128,1,1152]{2,1,0:T(1,128)}), f32[128,1,1152]{2,1,0:T(1,128)S(1)}, u32[]{:S(2)}, u32[]{:S(2)}) async-start(f32[128,1,1152]{2,1,0:T(1,128)} %bitcast.19), calls=%async_computation | async-start | bytes 1179648 | tf_op jit(solution)/shard_map/all_to_all | solution.py:418
  68.4 18.6 %collective-permute-start.11 = (s32[512,128]{1,0:T(8,128)S(1)}, s32[512,128]{1,0:T(8,128)S(1)}, u32[]{:S(2)}, u32[]{:S(2)}) collective-permute-start(s32[512,128]{1,0:T(8,128)S(1)} %copy.29), channel_id=1, source_target_pairs={{0,127},{1,126},{2,125},{3,124},{4,123},{5,122},{6,121},{7,120},{8... | collective-permute-start | bytes 786440 | tf_op jit(solution)/shard_map/ppermute | solution.py:484
  76.6 38.9 %copy-start.4 = (bf16[512,256]{1,0:T(8,128)(2,1)S(1)}, bf16[512,256]{1,0:T(8,128)(2,1)}, u32[]{:S(2)}) copy-start(bf16[512,256]{1,0:T(8,128)(2,1)} %constant.78.clone.table_ref) | copy-start | bytes 786436

commit v4 on v3

--- a/solution.py
+++ b/solution.py
@@ -448,12 +448,14 @@
         got = lax.dynamic_slice(source, (0, half, 0, EARLY), (4, 1, rows, length - EARLY))
         return got[:, 0] * weight
 
-    far_up = along(early(blocks, 2, 0), 1)
-    far_down = along(early(blocks, 2, 1), -1)
-    late_sent = late_block(blocks, 1 - upper)
+    far_pieces = early(blocks, 2, 0), early(blocks, 2, 1)
+    far_up = along(far_pieces[0], 1)
+    far_down = along(far_pieces[1], -1)
+    behind = after(blocks, far_pieces[0])
+    late_sent = late_block(behind, 1 - upper)
     late_other = swapped(late_sent)
-    up_free = along(early(blocks, 1, 1), 1)
-    down_free = along(early(blocks, -1, 0), -1)
+    up_free = along(early(behind, 1, 1), 1)
+    down_free = along(early(behind, -1, 0), -1)
     up_bound = along(early(after(blocks, far_up), 1, 0) + far_up, 1)
     down_bound = along(early(after(blocks, far_down), -1, 1) + far_down, -1)
     late = late_block(after(blocks, late_other), upper) + late_other
@@ -494,7 +496,7 @@
     bins = tiled(columns[: SHORT // 2])
     middle = columns[SHORT // 2].reshape(SHORT, LONG).T
     middle = jnp.pad(middle, ((0, 0), (0, 3 * SHORT)))
-    mirror = swapped_mirror(after(mirrored, parts[1]))
+    mirror = swapped_mirror(mirrored)
     sent = call(
         rows_forth_kernel,
         f32(LONG * FORTH, LONG),

time: 118 us -> 119 us (level)
  waiting for transfers between devices: 28.2 us -> 24.4 us
  starting transfers between devices: 41.8 us -> 45.3 us
  other arithmetic: 9 us -> 10.5 us
    ppermute x9, waiting for transfers between devices: 11.7 us -> 8.53 us  [along(): lax.ppermute(array, PLANES[0], [(i, (i + step) % 4) for i in range(4)])]
    ppermute x9, starting transfers between devices: 10.8 us -> 13.3 us  [along(): lax.ppermute(array, PLANES[0], [(i, (i + step) % 4) for i in range(4)])]
    mul x1 -> x2, other arithmetic: 1.38 us -> 3.09 us  [early(): return got[0] * weight]
  transfers between devices with their start and end apart: 13 -> 13, of which waited for: 6 -> 6; matrix products, arithmetic and copies ran while one was open for 11% -> 12% of each run, Pallas kernels for 0% -> 0%
where the time goes in v4:
time: 119 us
  starting transfers between devices  45.3 us (38%)
  waiting for transfers between devices  24.4 us (21%)
  blocking collectives  24.4 us (21%)
  other arithmetic  10.5 us (9%)
  Pallas kernels  7.35 us (6%)
  local copies, waits for them, and re-layouts  5.08 us (4%)
  between operations  1.54 us (1%)
    all_to_all x1, blocking collectives, exchanged(): lax.all_to_all(blocks, ROWS_PLANES, split_axis=0, concat_axis=0, tiled=True)  24.4 us
    all_to_all x1, starting transfers between devices, exchanged(): lax.all_to_all(blocks, ROWS_PLANES, split_axis=0, concat_axis=0, tiled=True)  16.6 us
    ppermute x9, starting transfers between devices, along(): lax.ppermute(array, PLANES[0], [(i, (i + step) % 4) for i in range(4)])  13.3 us
    ppermute x1, waiting for transfers between devices, swapped_mirror(): lax.ppermute(array, ROWS_PLANES, [(i, LONG - 1 - i) for i in range(LONG)])  10 us
    ppermute x9, waiting for transfers between devices, along(): lax.ppermute(array, PLANES[0], [(i, (i + step) % 4) for i in range(4)])  8.53 us
    ppermute x1, starting transfers between devices, swapped_mirror(): lax.ppermute(array, ROWS_PLANES, [(i, LONG - 1 - i) for i in range(LONG)])  8.05 us
    ppermute x2, starting transfers between devices, swapped(): return lax.ppermute(array, PLANES[1], [(0, 1), (1, 0)])  7.35 us
    pallas_call x3, Pallas kernels, call(): pl.pallas_call(kernel, out_shape=outs, in_specs=specs, out_specs=jax.tree...  7.35 us
  transfers between devices with their start and end apart: 13, of which 6 were waited for; matrix products, arithmetic and copies ran while one was open for 12% of the time, Pallas kernels for 0%

profile of v4, /device:TPU:1, one launch (start us, length us, event | category | flops | bytes accessed | tf_op | source)
XLA Modules:
  0.0 118.6 jit_solution(2858180213530158478)
XLA Ops:
  1.3 1.1 multiply_bitcast_fusion.1
  2.4 3.6 %collective-permute-start.4 = (f32[2,32,1280]{2,1,0:T(8,128)S(1)}, f32[2,32,1280]{2,1,0:T(8,128)S(1)}, u32[]{:S(2)}, u32[]{:S(2)}) collective-permute-start(f32[2,32,1280]{2,1,0:T(8,128)S(1)} %get-tuple-element.23), channel_id=1, source_target_pairs={{0,6},{2,0},{4,2},{6,4},{1,7},{3,1},{5,3},{7,5},{8,14},{10,8},{12,... | collective-permute-start | bytes 983048 | tf_op jit(solution)/shard_map/ppermute | solution.py:423
  6.0 2.0 %multiply_bitcast_fusion.2 = (f32[2,32,1280]{2,1,0:T(8,128)}, f32[2,32,1280]{2,1,0:T(8,128)}) fusion(f32[4,2,32,4096]{3,2,1,0:T(8,128)} %bitcast.83, s32[]{:T(128)S(6)} %select_n.31, f32[]{:T(128)} %bitcast.77, s32[]{:T(128)S(6)} %select_n.33), kind=kLoop, calls=%fused_computation.17 | loop fusion | flops 163840 | bytes 1310732 | tf_op jit(solution)/shard_map/mul | solution.py:445
  8.0 2.7 %collective-permute-start.2 = (f32[2,32,1280]{2,1,0:T(8,128)}, f32[2,32,1280]{2,1,0:T(8,128)S(1)}, u32[]{:S(2)}, u32[]{:S(2)}) collective-permute-start(f32[2,32,1280]{2,1,0:T(8,128)} %get-tuple-element.22), channel_id=1, source_target_pairs={{0,6},{2,0},{4,2},{6,4},{1,7},{3,1},{5,3},{7,5},{8,14},{10,8},{12,... | collective-permute-start | bytes 983048 | tf_op jit(solution)/shard_map/ppermute | solution.py:423
  10.7 1.7 %collective-permute-done.4 = f32[2,32,1280]{2,1,0:T(8,128)S(1)} collective-permute-done((f32[2,32,1280]{2,1,0:T(8,128)S(1)}, f32[2,32,1280]{2,1,0:T(8,128)S(1)}, u32[]{:S(2)}, u32[]{:S(2)}) %collective-permute-start.4) | collective-permute-done | bytes 327712 | tf_op jit(solution)/shard_map/ppermute | solution.py:423
  12.4 1.7 %bitcast_add_fusion.1 = f32[2,32,1280]{2,1,0:T(8,128)} fusion(f32[2,32,1280]{2,1,0:T(8,128)S(1)} %collective-permute-done.4, f32[4,2,32,4096]{3,2,1,0:T(8,128)} %bitcast.84, s32[]{:T(128)S(6)} %select_n.33, f32[]{:T(128)} %bitcast.75), kind=kLoop, calls=%fused_computation.10 | loop fusion | flops 163840 | bytes 983048 | tf_op jit(solution)/shard_map/add | solution.py:460
  14.2 3.4 %collective-permute-start.5 = (f32[2,32,1280]{2,1,0:T(8,128)}, f32[2,32,1280]{2,1,0:T(8,128)S(1)}, u32[]{:S(2)}, u32[]{:S(2)}) collective-permute-start(f32[2,32,1280]{2,1,0:T(8,128)} %bitcast_add_fusion.1), channel_id=1, source_target_pairs={{0,6},{2,0},{4,2},{6,4},{1,7},{3,1},{5,3},{7,5},{8,14},{10,8},{12,... | collective-permute-start | bytes 983048 | tf_op jit(solution)/shard_map/ppermute | solution.py:423
  17.6 1.7 %bitcast_add_fusion.4 = f32[2,32,1280]{2,1,0:T(8,128)} fusion(f32[2,32,1280]{2,1,0:T(8,128)S(1)} %collective-permute-done, f32[4,2,32,4096]{3,2,1,0:T(8,128)} %bitcast.85, s32[]{:T(128)S(6)} %select_n.31, f32[]{:T(128)} %bitcast.72), kind=kLoop, calls=%fused_computation.15 | loop fusion | flops 163840 | bytes 983048 | tf_op jit(solution)/shard_map/add | solution.py:459
  19.3 1.2 %multiply_bitcast_fusion = f32[4,32,1536]{2,1,0:T(8,128)S(1)} fusion(s32[]{:T(128)S(6)} %select_n.35, f32[]{:T(128)} %bitcast.73, f32[4,2,32,4096]{3,2,1,0:T(8,128)} %bitcast.86), kind=kLoop, calls=%fused_computation.1 | loop fusion | flops 196608 | bytes 1573380 | tf_op jit(solution)/shard_map/mul | solution.py:449
  20.5 3.7 %collective-permute-start.7 = (f32[4,32,1536]{2,1,0:T(8,128)S(1)}, f32[4,32,1536]{2,1,0:T(8,128)S(1)}, u32[]{:S(2)}, u32[]{:S(2)}) collective-permute-start(f32[4,32,1536]{2,1,0:T(8,128)S(1)} %multiply_bitcast_fusion), channel_id=1, source_target_pairs={{0,1},{1,0},{2,3},{3,2},{4,5},{5,4},{6,7},{7,6},{8,9},{9,8},{10,11... | collective-permute-start | bytes 2359304 | tf_op jit(solution)/shard_map/ppermute | solution.py:427
  24.2 4.1 %collective-permute-done.1 = f32[2,32,1280]{2,1,0:T(8,128)} collective-permute-done((f32[2,32,1280]{2,1,0:T(8,128)}, f32[2,32,1280]{2,1,0:T(8,128)}, u32[]{:S(2)}, u32[]{:S(2)}) %collective-permute-start.1) | collective-permute-done | bytes 327712 | tf_op jit(solution)/shard_map/ppermute | solution.py:423
  28.3 1.3 %fusion.4 = (f32[2,32,1280]{2,1,0:T(8,128)S(1)}, f32[2,32,1280]{2,1,0:T(8,128)S(1)}) fusion(f32[2,32,1280]{2,1,0:T(8,128)S(1)} %collective-permute-done.5, f32[2,32,1280]{2,1,0:T(8,128)S(1)} %collective-permute-done.3, f32[4,2,32,4096]{3,2,1,0:T(8,128)} %bitcast.87, s32[]{:T(128)S(6)} %select_n.32, f32[]{:T(128)} %bitcast.78, ...), kind=kLoop, calls=%fused_computation.12 | loop fusion | flops 491520 | bytes 2621448 | tf_op jit(solution)/shard_map/add | solution.py:471
  29.7 3.7 %collective-permute-start.6 = (f32[32,2560]{1,0:T(8,128)S(1)}, f32[32,2560]{1,0:T(8,128)S(1)}, u32[]{:S(2)}, u32[]{:S(2)}) collective-permute-start(f32[32,2560]{1,0:T(8,128)S(1)} %get-tuple-element.29), channel_id=1, source_target_pairs={{0,1},{1,0},{2,3},{3,2},{4,5},{5,4},{6,7},{7,6},{8,9},{9,8},{10,11... | collective-permute-start | bytes 983048 | tf_op jit(solution)/shard_map/ppermute | solution.py:427
  33.4 5.8 %collective-permute-done.7 = f32[4,32,1536]{2,1,0:T(8,128)S(1)} collective-permute-done((f32[4,32,1536]{2,1,0:T(8,128)S(1)}, f32[4,32,1536]{2,1,0:T(8,128)S(1)}, u32[]{:S(2)}, u32[]{:S(2)}) %collective-permute-start.7) | collective-permute-done | bytes 786464 | tf_op jit(solution)/shard_map/ppermute | solution.py:427
  39.2 1.2 %bitcast_add_fusion = f32[4,32,1536]{2,1,0:T(8,128)S(1)} fusion(f32[4,32,1536]{2,1,0:T(8,128)S(1)} %collective-permute-done.7, s32[]{:T(128)S(6)} %select_n.34, f32[]{:T(128)} %bitcast.74, f32[4,2,32,4096]{3,2,1,0:T(8,128)} %bitcast.88), kind=kLoop, calls=%fused_computation | loop fusion | flops 393216 | bytes 2359812 | tf_op jit(solution)/shard_map/add | solution.py:461
  40.4 0.8 dynamic-slice_bitcast_fusion
  41.2 2.7 %collective-permute-start.9 = (f32[32,1536]{1,0:T(8,128)}, f32[32,1536]{1,0:T(8,128)S(1)}, u32[]{:S(2)}, u32[]{:S(2)}) collective-permute-start(f32[32,1536]{1,0:T(8,128)} %get-tuple-element.26), channel_id=1, source_target_pairs={{0,6},{2,0},{4,2},{6,4},{1,7},{3,1},{5,3},{7,5},{8,14},{10,8},{12,... | collective-permute-start | bytes 589832 | tf_op jit(solution)/shard_map/ppermute | solution.py:423
  43.9 0.9 collective-permute-start.10
  45.0 2.3 %reverse.2 = s32[15,4096]{1,0:T(8,128)S(1)} reverse(s32[15,4096]{1,0:T(8,128)S(1)} %bitcast.89), dimensions={1} | reverse | bytes 491520
  47.3 0.2 slice.36
  47.5 1.5 %collective-permute-done.9.refs_4_ = f32[32,1536]{1,0:T(8,128)S(1)} collective-permute-done((f32[32,1536]{1,0:T(8,128)}, f32[32,1536]{1,0:T(8,128)S(1)}, u32[]{:S(2)}, u32[]{:S(2)}) %collective-permute-start.9) | collective-permute-done | bytes 196640 | tf_op jit(solution)/shard_map/ppermute | solution.py:423
  49.0 1.2 %collective-permute-done.10.refs_5_ = f32[32,1536]{1,0:T(8,128)S(1)} collective-permute-done((f32[32,1536]{1,0:T(8,128)S(1)}, f32[32,1536]{1,0:T(8,128)S(1)}, u32[]{:S(2)}, u32[]{:S(2)}) %collective-permute-start.10) | collective-permute-done | bytes 196640 | tf_op jit(solution)/shard_map/ppermute | solution.py:423
  50.2 1.5 %shard_map.121 = f32[1152,128]{1,0:T(8,128)} custom-call(f32[32,2560]{1,0:T(8,128)S(1)} %get-tuple-element.30.refs_0_, f32[32,2560]{1,0:T(8,128)S(1)} %collective-permute-done.6.refs_1_, f32[32,1536]{1,0:T(8,128)S(1)} %get-tuple-element.28.refs_2_, f32[32,1536]{1,0:T(8,128)S(1)} %collective-permute-done.8.refs_3_, ...), custom_call_target="tpu_custom_call" | custom-call | tf_op jit(solution)/shard_map/pallas_call | solution.py:402
  51.7 16.6 %all-to-all-start = ((f32[128,1,1152]{2,1,0:T(1,128)}), f32[128,1,1152]{2,1,0:T(1,128)S(1)}, u32[]{:S(2)}, u32[]{:S(2)}) async-start(f32[128,1,1152]{2,1,0:T(1,128)} %bitcast.19), calls=%async_computation | async-start | bytes 1179648 | tf_op jit(solution)/shard_map/all_to_all | solution.py:418
  68.4 0.8 rev.4
  69.3 0.2 copy.28
  69.6 8.1 %collective-permute-start.11 = (s32[512,128]{1,0:T(8,128)S(1)}, s32[512,128]{1,0:T(8,128)S(1)}, u32[]{:S(2)}, u32[]{:S(2)}) collective-permute-start(s32[512,128]{1,0:T(8,128)S(1)} %copy.29), channel_id=1, source_target_pairs={{0,127},{1,126},{2,125},{3,124},{4,123},{5,122},{6,121},{7,120},{8... | collective-permute-start | bytes 786440 | tf_op jit(solution)/shard_map/ppermute | solution.py:486
  77.8 0.2 copy.27
  78.2 10.0 %collective-permute-done.11.mirror_ref = s32[512,128]{1,0:T(8,128)S(1)} collective-permute-done((s32[512,128]{1,0:T(8,128)S(1)}, s32[512,128]{1,0:T(8,128)S(1)}, u32[]{:S(2)}, u32[]{:S(2)}) %collective-permute-start.11) | collective-permute-done | bytes 262176 | tf_op jit(solution)/shard_map/ppermute | solution.py:486
  88.3 4.0 %shard_map.122 = f32[2176,128]{1,0:T(8,128)S(1)} custom-call(s32[1]{0:T(128)} %bitcast.first_ref, f32[1152,128]{1,0:T(8,128)S(1)} %bitcast.81, s32[512,128]{1,0:T(8,128)S(1)} %copy.31.bins_ref, s32[512,128]{1,0:T(8,128)S(1)} %collective-permute-done.11.mirror_ref, s32[128,128]{1,0:T(8,128)S(1)} %pad.4.middle_ref, f32[2,128,128]{2,1,0:T(8,128)S(1)} %copy-done.6, ...), custom_call_target="tpu_custom_call" | custom-call | tf_op jit(solution)/shard_map/pallas_call | solution.py:402
  92.2 24.4 %all_to_all.10 = f32[128,1,2176]{2,1,0:T(1,128)S(1)} all-to-all(f32[128,1,2176]{2,1,0:T(1,128)S(1)} %bitcast.80), channel_id=1, replica_groups=mesh['rows_0'=4,'rows_1'=2,'rows_2'=2,'planes_0'=4,'planes_1'=2] {'rows_..., dimensions={0} | all-to-all | bytes 2228224 | tf_op jit(solution)/shard_map/all_to_all | solution.py:418
  116.7 1.9 %shard_map.123 = (f32[32,4096]{1,0:T(8,128)}, f32[32,4096]{1,0:T(8,128)}, f32[1,64]{1,0:T(1,128)}) custom-call(f32[2176,128]{1,0:T(8,128)S(1)} %bitcast.79, f32[2,32,128]{2,1,0:T(8,128)S(1)} %copy-done.5, bf16[512,256]{1,0:T(8,128)(2,1)S(1)} %copy-done.4), custom_call_target="tpu_custom_call" | custom-call | tf_op jit(solution)/shard_map/pallas_call | solution.py:402
  (42 shorter events, 1.0 us)
Async XLA Ops:
  2.4 10.0 %collective-permute-start.4 = (f32[2,32,1280]{2,1,0:T(8,128)S(1)}, f32[2,32,1280]{2,1,0:T(8,128)S(1)}, u32[]{:S(2)}, u32[]{:S(2)}) collective-permute-start(f32[2,32,1280]{2,1,0:T(8,128)S(1)} %get-tuple-element.23), channel_id=1, source_target_pairs={{0,6},{2,0},{4,2},{6,4},{1,7},{3,1},{5,3},{7,5},{8,14},{10,8},{12,... | collective-permute-start | bytes 983048 | tf_op jit(solution)/shard_map/ppermute | solution.py:423
  6.0 11.5 %collective-permute-start = (f32[2,32,1280]{2,1,0:T(8,128)S(1)}, f32[2,32,1280]{2,1,0:T(8,128)S(1)}, u32[]{:S(2)}, u32[]{:S(2)}) collective-permute-start(f32[2,32,1280]{2,1,0:T(8,128)S(1)} %get-tuple-element.24), channel_id=1, source_target_pairs={{0,2},{2,4},{4,6},{6,0},{1,3},{3,5},{5,7},{7,1},{8,10},{10,12},{12... | collective-permute-start | bytes 983048 | tf_op jit(solution)/shard_map/ppermute | solution.py:423
  8.0 20.3 %collective-permute-start.3 = (f32[2,32,1280]{2,1,0:T(8,128)}, f32[2,32,1280]{2,1,0:T(8,128)S(1)}, u32[]{:S(2)}, u32[]{:S(2)}) collective-permute-start(f32[2,32,1280]{2,1,0:T(8,128)} %get-tuple-element.21), channel_id=1, source_target_pairs={{0,2},{2,4},{4,6},{6,0},{1,3},{3,5},{5,7},{7,1},{8,10},{10,12},{12... | collective-permute-start | bytes 983048 | tf_op jit(solution)/shard_map/ppermute | solution.py:423
  8.0 20.2 %collective-permute-start.2 = (f32[2,32,1280]{2,1,0:T(8,128)}, f32[2,32,1280]{2,1,0:T(8,128)S(1)}, u32[]{:S(2)}, u32[]{:S(2)}) collective-permute-start(f32[2,32,1280]{2,1,0:T(8,128)} %get-tuple-element.22), channel_id=1, source_target_pairs={{0,6},{2,0},{4,2},{6,4},{1,7},{3,1},{5,3},{7,5},{8,14},{10,8},{12,... | collective-permute-start | bytes 983048 | tf_op jit(solution)/shard_map/ppermute | solution.py:423
  14.2 14.1 %collective-permute-start.5 = (f32[2,32,1280]{2,1,0:T(8,128)}, f32[2,32,1280]{2,1,0:T(8,128)S(1)}, u32[]{:S(2)}, u32[]{:S(2)}) collective-permute-start(f32[2,32,1280]{2,1,0:T(8,128)} %bitcast_add_fusion.1), channel_id=1, source_target_pairs={{0,6},{2,0},{4,2},{6,4},{1,7},{3,1},{5,3},{7,5},{8,14},{10,8},{12,... | collective-permute-start | bytes 983048 | tf_op jit(solution)/shard_map/ppermute | solution.py:423
  19.3 9.0 %collective-permute-start.1 = (f32[2,32,1280]{2,1,0:T(8,128)}, f32[2,32,1280]{2,1,0:T(8,128)}, u32[]{:S(2)}, u32[]{:S(2)}) collective-permute-start(f32[2,32,1280]{2,1,0:T(8,128)} %bitcast_add_fusion.4), channel_id=1, source_target_pairs={{0,2},{2,4},{4,6},{6,0},{1,3},{3,5},{5,7},{7,1},{8,10},{10,12},{12... | collective-permute-start | bytes 983048 | tf_op jit(solution)/shard_map/ppermute | solution.py:423
  20.5 24.3 %copy-start.7 = (s32[4096,32]{0,1:T(8,128)S(1)}, s32[4096,32]{0,1:T(8,128)}, u32[]{:S(2)}) copy-start(s32[4096,32]{0,1:T(8,128)} %param.12) | copy-start | bytes 1572868
  20.5 18.7 %collective-permute-start.7 = (f32[4,32,1536]{2,1,0:T(8,128)S(1)}, f32[4,32,1536]{2,1,0:T(8,128)S(1)}, u32[]{:S(2)}, u32[]{:S(2)}) collective-permute-start(f32[4,32,1536]{2,1,0:T(8,128)S(1)} %multiply_bitcast_fusion), channel_id=1, source_target_pairs={{0,1},{1,0},{2,3},{3,2},{4,5},{5,4},{6,7},{7,6},{8,9},{9,8},{10,11... | collective-permute-start | bytes 2359304 | tf_op jit(solution)/shard_map/ppermute | solution.py:427
  28.3 21.9 %copy-start = (bf16[256,512]{1,0:T(8,128)(2,1)S(1)}, bf16[256,512]{1,0:T(8,128)(2,1)}, u32[]{:S(2)}) copy-start(bf16[256,512]{1,0:T(8,128)(2,1)} %constant.73.clone.refs_7_.forth_ref) | copy-start | bytes 786436
  28.3 21.9 %copy-start.5 = (f32[2,32,128]{2,1,0:T(8,128)S(1)}, f32[2,32,128]{2,1,0:T(8,128)}, u32[]{:S(2)}) copy-start(f32[2,32,128]{2,1,0:T(8,128)} %constant.72.clone.refs_6_.turn_ref) | copy-start | bytes 98308
  29.7 17.8 %collective-permute-start.6 = (f32[32,2560]{1,0:T(8,128)S(1)}, f32[32,2560]{1,0:T(8,128)S(1)}, u32[]{:S(2)}, u32[]{:S(2)}) collective-permute-start(f32[32,2560]{1,0:T(8,128)S(1)} %get-tuple-element.29), channel_id=1, source_target_pairs={{0,1},{1,0},{2,3},{3,2},{4,5},{5,4},{6,7},{7,6},{8,9},{9,8},{10,11... | collective-permute-start | bytes 983048 | tf_op jit(solution)/shard_map/ppermute | solution.py:427
  41.2 6.2 %collective-permute-start.8 = (f32[32,1536]{1,0:T(8,128)}, f32[32,1536]{1,0:T(8,128)S(1)}, u32[]{:S(2)}, u32[]{:S(2)}) collective-permute-start(f32[32,1536]{1,0:T(8,128)} %get-tuple-element.27), channel_id=1, source_target_pairs={{0,2},{2,4},{4,6},{6,0},{1,3},{3,5},{5,7},{7,1},{8,10},{10,12},{12... | collective-permute-start | bytes 589832 | tf_op jit(solution)/shard_map/ppermute | solution.py:423
  41.2 7.7 %collective-permute-start.9 = (f32[32,1536]{1,0:T(8,128)}, f32[32,1536]{1,0:T(8,128)S(1)}, u32[]{:S(2)}, u32[]{:S(2)}) collective-permute-start(f32[32,1536]{1,0:T(8,128)} %get-tuple-element.26), channel_id=1, source_target_pairs={{0,6},{2,0},{4,2},{6,4},{1,7},{3,1},{5,3},{7,5},{8,14},{10,8},{12,... | collective-permute-start | bytes 589832 | tf_op jit(solution)/shard_map/ppermute | solution.py:423
  43.9 6.3 %collective-permute-start.10 = (f32[32,1536]{1,0:T(8,128)S(1)}, f32[32,1536]{1,0:T(8,128)S(1)}, u32[]{:S(2)}, u32[]{:S(2)}) collective-permute-start(f32[32,1536]{1,0:T(8,128)S(1)} %get-tuple-element.25), channel_id=1, source_target_pairs={{0,4},{2,6},{4,0},{6,2},{1,5},{3,7},{5,1},{7,3},{8,12},{10,14},{12... | collective-permute-start | bytes 589832 | tf_op jit(solution)/shard_map/ppermute | solution.py:423
  51.7 36.6 %copy-start.1 = (bf16[256,512]{1,0:T(8,128)(2,1)S(1)}, bf16[256,512]{1,0:T(8,128)(2,1)}, u32[]{:S(2)}) copy-start(bf16[256,512]{1,0:T(8,128)(2,1)} %constant.75.clone.back_ref) | copy-start | bytes 786436
  51.7 36.6 %copy-start.2 = (bf16[512,256]{1,0:T(8,128)(2,1)S(1)}, bf16[512,256]{1,0:T(8,128)(2,1)}, u32[]{:S(2)}) copy-start(bf16[512,256]{1,0:T(8,128)(2,1)} %constant.76.clone.short_forth_ref) | copy-start | bytes 786436
  51.7 36.6 %copy-start.3 = (bf16[512,256]{1,0:T(8,128)(2,1)S(1)}, bf16[512,256]{1,0:T(8,128)(2,1)}, u32[]{:S(2)}) copy-start(bf16[512,256]{1,0:T(8,128)(2,1)} %constant.77.clone.short_back_ref) | copy-start | bytes 786436
  51.7 36.6 %copy-start.6 = (f32[2,128,128]{2,1,0:T(8,128)S(1)}, f32[2,128,128]{2,1,0:T(8,128)}, u32[]{:S(2)}) copy-start(f32[2,128,128]{2,1,0:T(8,128)} %constant.74.clone.turn_ref) | copy-start | bytes 393220
  51.7 36.5 %all-to-all-start = ((f32[128,1,1152]{2,1,0:T(1,128)}), f32[128,1,1152]{2,1,0:T(1,128)S(1)}, u32[]{:S(2)}, u32[]{:S(2)}) async-start(f32[128,1,1152]{2,1,0:T(1,128)} %bitcast.19), calls=%async_computation | async-start | bytes 1179648 | tf_op jit(solution)/shard_map/all_to_all | solution.py:418
  69.6 18.6 %collective-permute-start.11 = (s32[512,128]{1,0:T(8,128)S(1)}, s32[512,128]{1,0:T(8,128)S(1)}, u32[]{:S(2)}, u32[]{:S(2)}) collective-permute-start(s32[512,128]{1,0:T(8,128)S(1)} %copy.29), channel_id=1, source_target_pairs={{0,127},{1,126},{2,125},{3,124},{4,123},{5,122},{6,121},{7,120},{8... | collective-permute-start | bytes 786440 | tf_op jit(solution)/shard_map/ppermute | solution.py:486
  77.7 39.0 %copy-start.4 = (bf16[512,256]{1,0:T(8,128)(2,1)S(1)}, bf16[512,256]{1,0:T(8,128)(2,1)}, u32[]{:S(2)}) copy-start(bf16[512,256]{1,0:T(8,128)(2,1)} %constant.78.clone.table_ref) | copy-start | bytes 786436

commit v5 on v4

--- a/solution.py
+++ b/solution.py
@@ -19,7 +19,7 @@
 ROWS_PLANES = ROWS + PLANES
 FORTH = 9
 BACK = 17
-EARLY_HALF = 1280
+EARLY_HALF = 1152
 EARLY = 2 * EARLY_HALF
 BF16 = jnp.bfloat16
 
@@ -448,11 +448,12 @@
         got = lax.dynamic_slice(source, (0, half, 0, EARLY), (4, 1, rows, length - EARLY))
         return got[:, 0] * weight
 
-    far_pieces = early(blocks, 2, 0), early(blocks, 2, 1)
+    late_sent = late_block(blocks, 1 - upper)
+    front = after(blocks, late_sent)
+    far_pieces = early(front, 2, 0), early(front, 2, 1)
     far_up = along(far_pieces[0], 1)
     far_down = along(far_pieces[1], -1)
     behind = after(blocks, far_pieces[0])
-    late_sent = late_block(behind, 1 - upper)
     late_other = swapped(late_sent)
     up_free = along(early(behind, 1, 1), 1)
     down_free = along(early(behind, -1, 0), -1)
@@ -489,7 +490,7 @@
 def on_device(density, lens_weight, spectrum_bin):
     held = tables()
     device = lax.axis_index(ROWS_PLANES)
-    parts = plane_sum(density[0], lens_weight[0])
+    parts = plane_sum(density[0], lens_weight.reshape(1, 1, 1))
     columns = spectrum_bin.T
     mirrored = jnp.roll(columns[SHORT // 2 + 1 :, ::-1], 1, axis=1)[::-1]
     mirrored = tiled(jnp.concatenate([columns[:1], mirrored], axis=0))

time: 119 us -> 124 us (1.042)
  waiting for transfers between devices: 24.4 us -> 30.4 us
    ppermute x2, waiting for transfers between devices: 5.83 us -> 9.08 us  [swapped(): return lax.ppermute(array, PLANES[1], [(0, 1), (1, 0)])]
    ppermute x9, waiting for transfers between devices: 8.53 us -> 11.3 us  [along(): lax.ppermute(array, PLANES[0], [(i, (i + step) % 4) for i in range(4)])]
    ppermute x9, starting transfers between devices: 13.3 us -> 11.8 us  [along(): lax.ppermute(array, PLANES[0], [(i, (i + step) % 4) for i in range(4)])]
  transfers between devices with their start and end apart: 13 -> 13, of which waited for: 6 -> 8; matrix products, arithmetic and copies ran while one was open for 12% -> 10% of each run, Pallas kernels for 0% -> 0%
where the time goes in v5:
time: 124 us; the launch traced here: 123 us
  starting transfers between devices  44.9 us (36%)
  waiting for transfers between devices  30.4 us (25%)
  blocking collectives  24.4 us (20%)
  other arithmetic  9.75 us (8%)
  Pallas kernels  7.35 us (6%)
  local copies, waits for them, and re-layouts  5.1 us (4%)
  between operations  1.52 us (1%)
    all_to_all x1, blocking collectives, exchanged(): lax.all_to_all(blocks, ROWS_PLANES, split_axis=0, concat_axis=0, tiled=True)  24.4 us
    all_to_all x1, starting transfers between devices, exchanged(): lax.all_to_all(blocks, ROWS_PLANES, split_axis=0, concat_axis=0, tiled=True)  17.8 us
    ppermute x9, starting transfers between devices, along(): lax.ppermute(array, PLANES[0], [(i, (i + step) % 4) for i in range(4)])  11.8 us
    ppermute x9, waiting for transfers between devices, along(): lax.ppermute(array, PLANES[0], [(i, (i + step) % 4) for i in range(4)])  11.3 us
    ppermute x1, waiting for transfers between devices, swapped_mirror(): lax.ppermute(array, ROWS_PLANES, [(i, LONG - 1 - i) for i in range(LONG)])  10 us
    ppermute x2, waiting for transfers between devices, swapped(): return lax.ppermute(array, PLANES[1], [(0, 1), (1, 0)])  9.08 us
    ppermute x1, starting transfers between devices, swapped_mirror(): lax.ppermute(array, ROWS_PLANES, [(i, LONG - 1 - i) for i in range(LONG)])  8.05 us
    pallas_call x3, Pallas kernels, call(): pl.pallas_call(kernel, out_shape=outs, in_specs=specs, out_specs=jax.tree...  7.35 us
  transfers between devices with their start and end apart: 13, of which 8 were waited for; matrix products, arithmetic and copies ran while one was open for 10% of the time, Pallas kernels for 0%

profile of v5, /device:TPU:1, one launch (start us, length us, event | category | flops | bytes accessed | tf_op | source)
XLA Modules:
  0.0 123.5 jit_solution(9104803680641005183)
XLA Ops:
  1.3 1.3 %fusion = f32[4,32,1792]{2,1,0:T(8,128)S(1)} fusion(f32[4,2,32,4096]{3,2,1,0:T(8,128)} %bitcast.86, s32[]{:T(128)S(6)} %select_n.30, f32[]{:T(128)} %bitcast.76), kind=kLoop, calls=%fused_computation.1 | loop fusion | flops 229376 | bytes 1835016 | tf_op jit(solution)/shard_map/mul | solution.py:449
  2.6 1.1 multiply_bitcast_fusion
  3.7 3.6 %collective-permute-start.4 = (f32[2,32,1152]{2,1,0:T(8,128)S(1)}, f32[2,32,1152]{2,1,0:T(8,128)S(1)}, u32[]{:S(2)}, u32[]{:S(2)}) collective-permute-start(f32[2,32,1152]{2,1,0:T(8,128)S(1)} %get-tuple-element.25), channel_id=1, source_target_pairs={{0,6},{2,0},{4,2},{6,4},{1,7},{3,1},{5,3},{7,5},{8,14},{10,8},{12,... | collective-permute-start | bytes 884744 | tf_op jit(solution)/shard_map/ppermute | solution.py:423
  7.3 1.1 multiply_bitcast_fusion.1
  8.5 2.7 %collective-permute-start.2 = (f32[2,32,1152]{2,1,0:T(8,128)S(1)}, f32[2,32,1152]{2,1,0:T(8,128)}, u32[]{:S(2)}, u32[]{:S(2)}) collective-permute-start(f32[2,32,1152]{2,1,0:T(8,128)S(1)} %get-tuple-element.24), channel_id=1, source_target_pairs={{0,6},{2,0},{4,2},{6,4},{1,7},{3,1},{5,3},{7,5},{8,14},{10,8},{12,... | collective-permute-start | bytes 884744 | tf_op jit(solution)/shard_map/ppermute | solution.py:423
  11.2 1.8 %collective-permute-done.4 = f32[2,32,1152]{2,1,0:T(8,128)S(1)} collective-permute-done((f32[2,32,1152]{2,1,0:T(8,128)S(1)}, f32[2,32,1152]{2,1,0:T(8,128)S(1)}, u32[]{:S(2)}, u32[]{:S(2)}) %collective-permute-start.4) | collective-permute-done | bytes 294944 | tf_op jit(solution)/shard_map/ppermute | solution.py:423
  13.0 3.1 %collective-permute-done = f32[2,32,1152]{2,1,0:T(8,128)S(1)} collective-permute-done((f32[2,32,1152]{2,1,0:T(8,128)S(1)}, f32[2,32,1152]{2,1,0:T(8,128)S(1)}, u32[]{:S(2)}, u32[]{:S(2)}) %collective-permute-start) | collective-permute-done | bytes 294944 | tf_op jit(solution)/shard_map/ppermute | solution.py:423
  16.1 1.7 %bitcast_add_fusion.4 = f32[2,32,1152]{2,1,0:T(8,128)} fusion(f32[2,32,1152]{2,1,0:T(8,128)S(1)} %collective-permute-done, f32[4,2,32,4096]{3,2,1,0:T(8,128)} %bitcast.89, s32[]{:T(128)S(6)} %select_n.32, f32[]{:T(128)} %bitcast.77), kind=kLoop, calls=%fused_computation.16 | loop fusion | flops 147456 | bytes 884744 | tf_op jit(solution)/shard_map/add | solution.py:460
  17.8 1.7 %bitcast_add_fusion.1 = f32[2,32,1152]{2,1,0:T(8,128)} fusion(f32[2,32,1152]{2,1,0:T(8,128)S(1)} %collective-permute-done.4, f32[4,2,32,4096]{3,2,1,0:T(8,128)} %bitcast.90, s32[]{:T(128)S(6)} %select_n.34, f32[]{:T(128)} %bitcast.79), kind=kLoop, calls=%fused_computation.11 | loop fusion | flops 147456 | bytes 884744 | tf_op jit(solution)/shard_map/add | solution.py:461
  19.5 2.7 %collective-permute-start.5 = (f32[2,32,1152]{2,1,0:T(8,128)}, f32[2,32,1152]{2,1,0:T(8,128)}, u32[]{:S(2)}, u32[]{:S(2)}) collective-permute-start(f32[2,32,1152]{2,1,0:T(8,128)} %bitcast_add_fusion.1), channel_id=1, source_target_pairs={{0,6},{2,0},{4,2},{6,4},{1,7},{3,1},{5,3},{7,5},{8,14},{10,8},{12,... | collective-permute-start | bytes 884744 | tf_op jit(solution)/shard_map/ppermute | solution.py:423
  22.2 3.6 %collective-permute-start.7 = (f32[4,32,1792]{2,1,0:T(8,128)S(1)}, f32[4,32,1792]{2,1,0:T(8,128)S(1)}, u32[]{:S(2)}, u32[]{:S(2)}) collective-permute-start(f32[4,32,1792]{2,1,0:T(8,128)S(1)} %fusion), channel_id=1, source_target_pairs={{0,1},{1,0},{2,3},{3,2},{4,5},{5,4},{6,7},{7,6},{8,9},{9,8},{10,11... | collective-permute-start | bytes 2752520 | tf_op jit(solution)/shard_map/ppermute | solution.py:427
  25.8 2.7 %collective-permute-done.1 = f32[2,32,1152]{2,1,0:T(8,128)} collective-permute-done((f32[2,32,1152]{2,1,0:T(8,128)}, f32[2,32,1152]{2,1,0:T(8,128)}, u32[]{:S(2)}, u32[]{:S(2)}) %collective-permute-start.1) | collective-permute-done | bytes 294944 | tf_op jit(solution)/shard_map/ppermute | solution.py:423
  28.5 1.4 %fusion.5 = (f32[2,32,1152]{2,1,0:T(8,128)S(1)}, f32[2,32,1152]{2,1,0:T(8,128)S(1)}) fusion(f32[2,32,1152]{2,1,0:T(8,128)} %collective-permute-done.5, f32[2,32,1152]{2,1,0:T(8,128)S(1)} %collective-permute-done.3, f32[4,2,32,4096]{3,2,1,0:T(8,128)} %bitcast.91, s32[]{:T(128)S(6)} %select_n.33, f32[]{:T(128)} %bitcast.82, ...), kind=kLoop, calls=%fused_computation.13 | loop fusion | flops 442368 | bytes 2359304 | tf_op jit(solution)/shard_map/add | solution.py:472
  30.0 3.7 %collective-permute-start.6 = (f32[32,2304]{1,0:T(8,128)S(1)}, f32[32,2304]{1,0:T(8,128)S(1)}, u32[]{:S(2)}, u32[]{:S(2)}) collective-permute-start(f32[32,2304]{1,0:T(8,128)S(1)} %get-tuple-element.31), channel_id=1, source_target_pairs={{0,1},{1,0},{2,3},{3,2},{4,5},{5,4},{6,7},{7,6},{8,9},{9,8},{10,11... | collective-permute-start | bytes 884744 | tf_op jit(solution)/shard_map/ppermute | solution.py:427
  33.7 9.1 %collective-permute-done.7 = f32[4,32,1792]{2,1,0:T(8,128)S(1)} collective-permute-done((f32[4,32,1792]{2,1,0:T(8,128)S(1)}, f32[4,32,1792]{2,1,0:T(8,128)S(1)}, u32[]{:S(2)}, u32[]{:S(2)}) %collective-permute-start.7) | collective-permute-done | bytes 917536 | tf_op jit(solution)/shard_map/ppermute | solution.py:427
  42.7 1.3 %bitcast_add_fusion = f32[4,32,1792]{2,1,0:T(8,128)S(1)} fusion(f32[4,32,1792]{2,1,0:T(8,128)S(1)} %collective-permute-done.7, s32[]{:T(128)S(6)} %select_n.35, f32[]{:T(128)} %bitcast.78, f32[4,2,32,4096]{3,2,1,0:T(8,128)} %bitcast.92), kind=kLoop, calls=%fused_computation.2 | loop fusion | flops 458752 | bytes 2753028 | tf_op jit(solution)/shard_map/add | solution.py:462
  44.0 0.8 dynamic-slice_bitcast_fusion
  44.9 2.7 %collective-permute-start.9 = (f32[32,1792]{1,0:T(8,128)}, f32[32,1792]{1,0:T(8,128)S(1)}, u32[]{:S(2)}, u32[]{:S(2)}) collective-permute-start(f32[32,1792]{1,0:T(8,128)} %get-tuple-element.28), channel_id=1, source_target_pairs={{0,6},{2,0},{4,2},{6,4},{1,7},{3,1},{5,3},{7,5},{8,14},{10,8},{12,... | collective-permute-start | bytes 688136 | tf_op jit(solution)/shard_map/ppermute | solution.py:423
  47.7 2.3 %reverse.2 = s32[15,4096]{1,0:T(8,128)S(1)} reverse(s32[15,4096]{1,0:T(8,128)S(1)} %bitcast.93), dimensions={1} | reverse | bytes 491520
  50.0 0.2 slice.36
  50.2 1.3 %collective-permute-done.8.refs_3_ = f32[32,1792]{1,0:T(8,128)S(1)} collective-permute-done((f32[32,1792]{1,0:T(8,128)}, f32[32,1792]{1,0:T(8,128)S(1)}, u32[]{:S(2)}, u32[]{:S(2)}) %collective-permute-start.8) | collective-permute-done | bytes 229408 | tf_op jit(solution)/shard_map/ppermute | solution.py:423
  51.4 1.8 %collective-permute-done.9.refs_4_ = f32[32,1792]{1,0:T(8,128)S(1)} collective-permute-done((f32[32,1792]{1,0:T(8,128)}, f32[32,1792]{1,0:T(8,128)S(1)}, u32[]{:S(2)}, u32[]{:S(2)}) %collective-permute-start.9) | collective-permute-done | bytes 229408 | tf_op jit(solution)/shard_map/ppermute | solution.py:423
  53.3 0.6 collective-permute-done.10.refs_5_
  53.9 1.5 %shard_map.121 = f32[1152,128]{1,0:T(8,128)} custom-call(f32[32,2304]{1,0:T(8,128)S(1)} %get-tuple-element.32.refs_0_, f32[32,2304]{1,0:T(8,128)S(1)} %collective-permute-done.6.refs_1_, f32[32,1792]{1,0:T(8,128)S(1)} %get-tuple-element.30.refs_2_, f32[32,1792]{1,0:T(8,128)S(1)} %collective-permute-done.8.refs_3_, ...), custom_call_target="tpu_custom_call" | custom-call | tf_op jit(solution)/shard_map/pallas_call | solution.py:402
  55.4 17.8 %all-to-all-start = ((f32[128,1,1152]{2,1,0:T(1,128)}), f32[128,1,1152]{2,1,0:T(1,128)S(1)}, u32[]{:S(2)}, u32[]{:S(2)}) async-start(f32[128,1,1152]{2,1,0:T(1,128)} %bitcast.19), calls=%async_computation | async-start | bytes 1179648 | tf_op jit(solution)/shard_map/all_to_all | solution.py:418
  73.3 0.8 rev.4
  74.2 0.2 copy.28
  74.5 8.1 %collective-permute-start.11 = (s32[512,128]{1,0:T(8,128)S(1)}, s32[512,128]{1,0:T(8,128)S(1)}, u32[]{:S(2)}, u32[]{:S(2)}) collective-permute-start(s32[512,128]{1,0:T(8,128)S(1)} %copy.29), channel_id=1, source_target_pairs={{0,127},{1,126},{2,125},{3,124},{4,123},{5,122},{6,121},{7,120},{8... | collective-permute-start | bytes 786440 | tf_op jit(solution)/shard_map/ppermute | solution.py:487
  83.1 10.0 %collective-permute-done.11.mirror_ref = s32[512,128]{1,0:T(8,128)S(1)} collective-permute-done((s32[512,128]{1,0:T(8,128)S(1)}, s32[512,128]{1,0:T(8,128)S(1)}, u32[]{:S(2)}, u32[]{:S(2)}) %collective-permute-start.11) | collective-permute-done | bytes 262176 | tf_op jit(solution)/shard_map/ppermute | solution.py:487
  93.2 4.0 %shard_map.122 = f32[2176,128]{1,0:T(8,128)S(1)} custom-call(s32[1]{0:T(128)} %bitcast.first_ref, f32[1152,128]{1,0:T(8,128)S(1)} %bitcast.85, s32[512,128]{1,0:T(8,128)S(1)} %copy.31.bins_ref, s32[512,128]{1,0:T(8,128)S(1)} %collective-permute-done.11.mirror_ref, s32[128,128]{1,0:T(8,128)S(1)} %pad.4.middle_ref, f32[2,128,128]{2,1,0:T(8,128)S(1)} %copy-done.6, ...), custom_call_target="tpu_custom_call" | custom-call | tf_op jit(solution)/shard_map/pallas_call | solution.py:402
  97.1 24.4 %all_to_all.10 = f32[128,1,2176]{2,1,0:T(1,128)S(1)} all-to-all(f32[128,1,2176]{2,1,0:T(1,128)S(1)} %bitcast.84), channel_id=1, replica_groups=mesh['rows_0'=4,'rows_1'=2,'rows_2'=2,'planes_0'=4,'planes_1'=2] {'rows_..., dimensions={0} | all-to-all | bytes 2228224 | tf_op jit(solution)/shard_map/all_to_all | solution.py:418
  121.6 1.9 %shard_map.123 = (f32[32,4096]{1,0:T(8,128)}, f32[32,4096]{1,0:T(8,128)}, f32[1,64]{1,0:T(1,128)}) custom-call(f32[2176,128]{1,0:T(8,128)S(1)} %bitcast.83, f32[2,32,128]{2,1,0:T(8,128)S(1)} %copy-done.5, bf16[512,256]{1,0:T(8,128)(2,1)S(1)} %copy-done.4), custom_call_target="tpu_custom_call" | custom-call | tf_op jit(solution)/shard_map/pallas_call | solution.py:402
  (42 shorter events, 1.2 us)
Async XLA Ops:
  3.7 9.3 %collective-permute-start.4 = (f32[2,32,1152]{2,1,0:T(8,128)S(1)}, f32[2,32,1152]{2,1,0:T(8,128)S(1)}, u32[]{:S(2)}, u32[]{:S(2)}) collective-permute-start(f32[2,32,1152]{2,1,0:T(8,128)S(1)} %get-tuple-element.25), channel_id=1, source_target_pairs={{0,6},{2,0},{4,2},{6,4},{1,7},{3,1},{5,3},{7,5},{8,14},{10,8},{12,... | collective-permute-start | bytes 884744 | tf_op jit(solution)/shard_map/ppermute | solution.py:423
  7.3 8.8 %collective-permute-start = (f32[2,32,1152]{2,1,0:T(8,128)S(1)}, f32[2,32,1152]{2,1,0:T(8,128)S(1)}, u32[]{:S(2)}, u32[]{:S(2)}) collective-permute-start(f32[2,32,1152]{2,1,0:T(8,128)S(1)} %get-tuple-element.26), channel_id=1, source_target_pairs={{0,2},{2,4},{4,6},{6,0},{1,3},{3,5},{5,7},{7,1},{8,10},{10,12},{12... | collective-permute-start | bytes 884744 | tf_op jit(solution)/shard_map/ppermute | solution.py:423
  8.4 20.1 %collective-permute-start.3 = (f32[2,32,1152]{2,1,0:T(8,128)S(1)}, f32[2,32,1152]{2,1,0:T(8,128)S(1)}, u32[]{:S(2)}, u32[]{:S(2)}) collective-permute-start(f32[2,32,1152]{2,1,0:T(8,128)S(1)} %get-tuple-element.23), channel_id=1, source_target_pairs={{0,2},{2,4},{4,6},{6,0},{1,3},{3,5},{5,7},{7,1},{8,10},{10,12},{12... | collective-permute-start | bytes 884744 | tf_op jit(solution)/shard_map/ppermute | solution.py:423
  8.5 20.0 %collective-permute-start.2 = (f32[2,32,1152]{2,1,0:T(8,128)S(1)}, f32[2,32,1152]{2,1,0:T(8,128)}, u32[]{:S(2)}, u32[]{:S(2)}) collective-permute-start(f32[2,32,1152]{2,1,0:T(8,128)S(1)} %get-tuple-element.24), channel_id=1, source_target_pairs={{0,6},{2,0},{4,2},{6,4},{1,7},{3,1},{5,3},{7,5},{8,14},{10,8},{12,... | collective-permute-start | bytes 884744 | tf_op jit(solution)/shard_map/ppermute | solution.py:423
  17.8 10.7 %collective-permute-start.1 = (f32[2,32,1152]{2,1,0:T(8,128)}, f32[2,32,1152]{2,1,0:T(8,128)}, u32[]{:S(2)}, u32[]{:S(2)}) collective-permute-start(f32[2,32,1152]{2,1,0:T(8,128)} %bitcast_add_fusion.4), channel_id=1, source_target_pairs={{0,2},{2,4},{4,6},{6,0},{1,3},{3,5},{5,7},{7,1},{8,10},{10,12},{12... | collective-permute-start | bytes 884744 | tf_op jit(solution)/shard_map/ppermute | solution.py:423
  19.5 28.0 %copy-start.7 = (s32[4096,32]{0,1:T(8,128)S(1)}, s32[4096,32]{0,1:T(8,128)}, u32[]{:S(2)}) copy-start(s32[4096,32]{0,1:T(8,128)} %param.12) | copy-start | bytes 1572868
  19.5 9.0 %collective-permute-start.5 = (f32[2,32,1152]{2,1,0:T(8,128)}, f32[2,32,1152]{2,1,0:T(8,128)}, u32[]{:S(2)}, u32[]{:S(2)}) collective-permute-start(f32[2,32,1152]{2,1,0:T(8,128)} %bitcast_add_fusion.1), channel_id=1, source_target_pairs={{0,6},{2,0},{4,2},{6,4},{1,7},{3,1},{5,3},{7,5},{8,14},{10,8},{12,... | collective-permute-start | bytes 884744 | tf_op jit(solution)/shard_map/ppermute | solution.py:423
  22.2 20.5 %collective-permute-start.7 = (f32[4,32,1792]{2,1,0:T(8,128)S(1)}, f32[4,32,1792]{2,1,0:T(8,128)S(1)}, u32[]{:S(2)}, u32[]{:S(2)}) collective-permute-start(f32[4,32,1792]{2,1,0:T(8,128)S(1)} %fusion), channel_id=1, source_target_pairs={{0,1},{1,0},{2,3},{3,2},{4,5},{5,4},{6,7},{7,6},{8,9},{9,8},{10,11... | collective-permute-start | bytes 2752520 | tf_op jit(solution)/shard_map/ppermute | solution.py:427
  29.9 24.0 %copy-start = (bf16[256,512]{1,0:T(8,128)(2,1)S(1)}, bf16[256,512]{1,0:T(8,128)(2,1)}, u32[]{:S(2)}) copy-start(bf16[256,512]{1,0:T(8,128)(2,1)} %constant.73.clone.refs_7_.forth_ref) | copy-start | bytes 786436
  29.9 24.0 %copy-start.5 = (f32[2,32,128]{2,1,0:T(8,128)S(1)}, f32[2,32,128]{2,1,0:T(8,128)}, u32[]{:S(2)}) copy-start(f32[2,32,128]{2,1,0:T(8,128)} %constant.72.clone.refs_6_.turn_ref) | copy-start | bytes 98308
  30.0 20.2 %collective-permute-start.6 = (f32[32,2304]{1,0:T(8,128)S(1)}, f32[32,2304]{1,0:T(8,128)S(1)}, u32[]{:S(2)}, u32[]{:S(2)}) collective-permute-start(f32[32,2304]{1,0:T(8,128)S(1)} %get-tuple-element.31), channel_id=1, source_target_pairs={{0,1},{1,0},{2,3},{3,2},{4,5},{5,4},{6,7},{7,6},{8,9},{9,8},{10,11... | collective-permute-start | bytes 884744 | tf_op jit(solution)/shard_map/ppermute | solution.py:427
  44.9 6.6 %collective-permute-start.8 = (f32[32,1792]{1,0:T(8,128)}, f32[32,1792]{1,0:T(8,128)S(1)}, u32[]{:S(2)}, u32[]{:S(2)}) collective-permute-start(f32[32,1792]{1,0:T(8,128)} %get-tuple-element.29), channel_id=1, source_target_pairs={{0,2},{2,4},{4,6},{6,0},{1,3},{3,5},{5,7},{7,1},{8,10},{10,12},{12... | collective-permute-start | bytes 688136 | tf_op jit(solution)/shard_map/ppermute | solution.py:423
  44.9 8.4 %collective-permute-start.9 = (f32[32,1792]{1,0:T(8,128)}, f32[32,1792]{1,0:T(8,128)S(1)}, u32[]{:S(2)}, u32[]{:S(2)}) collective-permute-start(f32[32,1792]{1,0:T(8,128)} %get-tuple-element.28), channel_id=1, source_target_pairs={{0,6},{2,0},{4,2},{6,4},{1,7},{3,1},{5,3},{7,5},{8,14},{10,8},{12,... | collective-permute-start | bytes 688136 | tf_op jit(solution)/shard_map/ppermute | solution.py:423
  47.5 6.4 %collective-permute-start.10 = (f32[32,1792]{1,0:T(8,128)S(1)}, f32[32,1792]{1,0:T(8,128)S(1)}, u32[]{:S(2)}, u32[]{:S(2)}) collective-permute-start(f32[32,1792]{1,0:T(8,128)S(1)} %get-tuple-element.27), channel_id=1, source_target_pairs={{0,4},{2,6},{4,0},{6,2},{1,5},{3,7},{5,1},{7,3},{8,12},{10,14},{12... | collective-permute-start | bytes 688136 | tf_op jit(solution)/shard_map/ppermute | solution.py:423
  55.4 37.8 %copy-start.1 = (bf16[256,512]{1,0:T(8,128)(2,1)S(1)}, bf16[256,512]{1,0:T(8,128)(2,1)}, u32[]{:S(2)}) copy-start(bf16[256,512]{1,0:T(8,128)(2,1)} %constant.75.clone.back_ref) | copy-start | bytes 786436
  55.4 37.8 %copy-start.2 = (bf16[512,256]{1,0:T(8,128)(2,1)S(1)}, bf16[512,256]{1,0:T(8,128)(2,1)}, u32[]{:S(2)}) copy-start(bf16[512,256]{1,0:T(8,128)(2,1)} %constant.76.clone.short_forth_ref) | copy-start | bytes 786436
  55.4 37.8 %copy-start.3 = (bf16[512,256]{1,0:T(8,128)(2,1)S(1)}, bf16[512,256]{1,0:T(8,128)(2,1)}, u32[]{:S(2)}) copy-start(bf16[512,256]{1,0:T(8,128)(2,1)} %constant.77.clone.short_back_ref) | copy-start | bytes 786436
  55.4 37.8 %copy-start.6 = (f32[2,128,128]{2,1,0:T(8,128)S(1)}, f32[2,128,128]{2,1,0:T(8,128)}, u32[]{:S(2)}) copy-start(f32[2,128,128]{2,1,0:T(8,128)} %constant.74.clone.turn_ref) | copy-start | bytes 393220
  55.4 37.7 %all-to-all-start = ((f32[128,1,1152]{2,1,0:T(1,128)}), f32[128,1,1152]{2,1,0:T(1,128)S(1)}, u32[]{:S(2)}, u32[]{:S(2)}) async-start(f32[128,1,1152]{2,1,0:T(1,128)} %bitcast.19), calls=%async_computation | async-start | bytes 1179648 | tf_op jit(solution)/shard_map/all_to_all | solution.py:418
  74.5 18.6 %collective-permute-start.11 = (s32[512,128]{1,0:T(8,128)S(1)}, s32[512,128]{1,0:T(8,128)S(1)}, u32[]{:S(2)}, u32[]{:S(2)}) collective-permute-start(s32[512,128]{1,0:T(8,128)S(1)} %copy.29), channel_id=1, source_target_pairs={{0,127},{1,126},{2,125},{3,124},{4,123},{5,122},{6,121},{7,120},{8... | collective-permute-start | bytes 786440 | tf_op jit(solution)/shard_map/ppermute | solution.py:487
  82.6 39.0 %copy-start.4 = (bf16[512,256]{1,0:T(8,128)(2,1)S(1)}, bf16[512,256]{1,0:T(8,128)(2,1)}, u32[]{:S(2)}) copy-start(bf16[512,256]{1,0:T(8,128)(2,1)} %constant.78.clone.table_ref) | copy-start | bytes 786436
